TPU v7x, 8 devices: a whole 2x2x1 slice. The times are simulated.
8 devices in a mesh: dp: 2 (over z, y), tp: 4 (over x, core).
Axes of the slice: x: 2, y: 2, z: 1, core: 2. Of those that a mesh axis runs over, the one named last changes fastest.
Arguments:
- hidden: bfloat16 [64, 512, 768], P('dp')
- positions: int32 [64, 80], P('dp')
- labels: int32 [64, 80], P('dp')
- weights: float32 [64, 80], P('dp')
- w_t: bfloat16 [768, 768], replicated
- b_t: float32 [768], replicated
- gamma: float32 [768], replicated
- beta: float32 [768], replicated
- embed: bfloat16 [30592, 768], P('tp')
- out_bias: float32 [30592], P('tp')
Outputs:
- output 1: float32 [], replicated
- output 2: bfloat16 [64, 512, 768], P('dp')
- output 3: float32 [768, 768], replicated
- output 4: float32 [768], replicated
- output 5: float32 [768], replicated
- output 6: float32 [768], replicated
- output 7: float32 [30592, 768], P('tp')
- output 8: float32 [30592], P('tp')
All inputs are finite; a program needn't handle non-finite values.
Results may differ from a plain program's by a relative error of at most 0.001.
Values sent between devices are 32-bit elements.
A program may use at most 1 GiB of HBM per device.

v0:
```python
import functools

import jax
import jax.numpy as jnp
from jax import lax
from jax.experimental import pallas as pl
from jax.experimental.pallas import tpu as pltpu
from jax.sharding import PartitionSpec as P

LN_EPS = 1e-12
LOSS_EPS = 1e-5
F32 = jnp.float32
BF16 = jnp.bfloat16
VT = 512
CB = 512
MAIN = 1536
CHUNKS = 2
CUT = 1024
SUB = 64
BACK = 256
WIN = 128
VMEM_LIMIT = 60 * 1024 * 1024

SWAP_DP = tuple((i, i ^ 1) for i in range(2))
SWAP_CORE = tuple((i, i ^ 1) for i in range(4))
SWAP_X = tuple((i, i ^ 2) for i in range(4))
FIRST, SECOND, THIRD = (slice(i, i + 1) for i in range(3))


def whole(*shape):
    return pl.BlockSpec(shape, lambda *_: (0,) * len(shape))


def swap_dp(x):
    return lax.ppermute(x, "dp", SWAP_DP)


def swap_core(x):
    return lax.ppermute(x, "tp", SWAP_CORE)


def swap_x(x):
    return lax.ppermute(x, "tp", SWAP_X)


def gather_body(per, meta_ref, idx_ref, h_ref, out_ref, acc):
    step = pl.program_id(0)

    @pl.when(step == 0)
    def _():
        acc[...] = jnp.zeros_like(acc)

    seq_len = h_ref.shape[1]
    lane = lax.broadcasted_iota(jnp.int32, (WIN, seq_len), 1).astype(F32)
    for i in range(per):
        col = jnp.broadcast_to(idx_ref[i], (WIN, WIN)).T
        hot = jnp.concatenate([col] * (seq_len // WIN), axis=1) == lane
        rows = jnp.dot(hot.astype(F32).astype(BF16), h_ref[i], preferred_element_type=F32)
        base = pl.multiple_of(meta_ref[step * per + i], 8)
        acc[pl.ds(base, WIN), :] += rows

    @pl.when(step == pl.num_programs(0) - 1)
    def _():
        out_ref[...] = acc[: out_ref.shape[0], :].astype(BF16)


def gather_pass(hidden, idx_win, base, rows):
    batch, seq_len, width = hidden.shape
    per = 4
    return pl.pallas_call(
        functools.partial(gather_body, per),
        out_shape=jax.ShapeDtypeStruct((rows, width), BF16),
        grid_spec=pltpu.PrefetchScalarGridSpec(
            num_scalar_prefetch=1, grid=(batch // per,),
            in_specs=[
                pl.BlockSpec((per, 1, WIN), lambda b, m: (b, 0, 0)),
                pl.BlockSpec((per, seq_len, width), lambda b, m: (b, 0, 0)),
            ],
            out_specs=whole(rows, width),
            scratch_shapes=[pltpu.VMEM((rows + WIN, width), F32)],
        ),
        compiler_params=pltpu.CompilerParams(dimension_semantics=("arbitrary",), vmem_limit_bytes=VMEM_LIMIT),
        cost_estimate=pl.CostEstimate(flops=2 * batch * WIN * seq_len * width, bytes_accessed=batch * seq_len * width * 2, transcendentals=0),
    )(base, idx_win, hidden)


def transform_body(meta_ref, h_ref, w_ref, vec_ref, t_ref, tt_ref, norm_ref, slope_ref, send_ref, pre, t_s):
    pre[...] = jnp.dot(h_ref[...], w_ref[...], preferred_element_type=F32) + vec_ref[FIRST]

    def some(i, _):
        at = pl.ds(pl.multiple_of(i * SUB, SUB), SUB)
        u = pre[at, :]
        cdf = 0.5 * (1.0 + lax.erf(u * 0.7071067811865476))
        act = u * cdf
        mean = jnp.mean(act, axis=1, keepdims=True)
        cent = act - mean
        inv = lax.rsqrt(jnp.mean(cent * cent, axis=1, keepdims=True) + LN_EPS)
        norm = cent * inv
        norm_ref[at, :] = norm
        slope_ref[at, :] = (cdf + u * (0.3989422804014327 * jnp.exp(-0.5 * u * u))) * inv
        t_s[at, :] = norm * vec_ref[SECOND] + vec_ref[THIRD]
        return 0

    lax.fori_loop(0, h_ref.shape[0] // SUB, some, 0)
    t = t_s[...].astype(BF16)
    t_ref[...] = t
    tt_ref[...] = t.T

    @pl.when(pl.program_id(0) == meta_ref[0])
    def _():
        send_ref[...] = t_s[...]


def transform_pass(h, w_t, vecs, tp, chunk):
    width = h.shape[1]
    part = MAIN // 4
    strip = pl.BlockSpec((part, width), lambda i, m: (i, 0))
    return pl.pallas_call(
        transform_body,
        out_shape=(
            jax.ShapeDtypeStruct((MAIN, width), BF16), jax.ShapeDtypeStruct((width, MAIN), BF16),
            jax.ShapeDtypeStruct((MAIN, width), F32), jax.ShapeDtypeStruct((MAIN, width), F32),
            jax.ShapeDtypeStruct((part, width), F32),
        ),
        grid_spec=pltpu.PrefetchScalarGridSpec(
            num_scalar_prefetch=1, grid=(4,),
            in_specs=[pl.BlockSpec((part, width), lambda i, m: (m[1] * 4 + i, 0)), whole(width, width), whole(8, width)],
            out_specs=(strip, pl.BlockSpec((width, part), lambda i, m: (0, i)), strip, strip, whole(part, width)),
            scratch_shapes=[pltpu.VMEM((part, width), F32), pltpu.VMEM((part, width), F32)],
        ),
        compiler_params=params(),
        cost_estimate=pl.CostEstimate(flops=2 * MAIN * width * width, bytes_accessed=MAIN * width * 14, transcendentals=2 * MAIN * width),
    )(jnp.stack([tp, chunk]), h, w_t, vecs)


def collect_body(place_ref, *refs):
    t_ref, tt_ref = refs[4:]
    for i, piece in enumerate(refs[:4]):
        @pl.when(pl.program_id(0) == i)
        def _():
            t = piece[...].astype(BF16)
            t_ref[...] = t
            tt_ref[...] = t.T


def collect_pass(pieces, tp):
    part, width = pieces[0].shape
    return pl.pallas_call(
        collect_body,
        out_shape=(jax.ShapeDtypeStruct((MAIN, width), BF16), jax.ShapeDtypeStruct((width, MAIN), BF16)),
        grid_spec=pltpu.PrefetchScalarGridSpec(
            num_scalar_prefetch=1, grid=(4,),
            in_specs=[whole(part, width)] * 4,
            out_specs=(pl.BlockSpec((part, width), lambda i, m: (m[i], 0)), pl.BlockSpec((width, part), lambda i, m: (0, m[i]))),
        ),
        compiler_params=params(),
        cost_estimate=pl.CostEstimate(flops=MAIN * width, bytes_accessed=MAIN * width * 8, transcendentals=0),
    )(tp ^ jnp.array([0, 2, 1, 3], jnp.int32), *pieces)


def back_body(meta_ref, mine_a_ref, theirs_a_ref, mine_b_ref, theirs_b_ref, norm_ref, slope_ref, h_ref, w_ref, gamma_ref, old_ref, dh_ref, pack_ref):
    step = pl.program_id(0)
    last = pl.num_programs(0) - 1
    width = w_ref.shape[0]

    @pl.when(step == 0)
    def _():
        pack_ref[...] = jnp.zeros_like(pack_ref)

    @pl.when(step < last)
    def _():
        low = meta_ref[0] == 0
        in_a = step < CUT // BACK
        mine = jnp.where(in_a, mine_a_ref[...], mine_b_ref[...]).T
        theirs = jnp.where(in_a, theirs_a_ref[...], theirs_b_ref[...]).T
        d_t = jnp.concatenate([jnp.where(low, mine, theirs), jnp.where(low, theirs, mine)], axis=1)
        norm = norm_ref[...]
        d_gamma = jnp.sum(d_t * norm, axis=0, keepdims=True)
        d_beta = jnp.sum(d_t, axis=0, keepdims=True)
        g = d_t * gamma_ref[...]
        g_mean = jnp.mean(g, axis=1, keepdims=True)
        gn_mean = jnp.mean(g * norm, axis=1, keepdims=True)
        d_u = (g - g_mean - norm * gn_mean) * slope_ref[...]
        d_b = jnp.sum(d_u, axis=0, keepdims=True)
        pack_ref[width:width + 8] += jnp.concatenate([d_b, d_gamma, d_beta] + [jnp.zeros_like(d_b)] * 5)
        d_u = d_u.astype(BF16)
        pack_ref[:width] += lax.dot_general(h_ref[...], d_u, (((0,), (0,)), ((), ())), preferred_element_type=F32)
        d_h = lax.dot_general(d_u, w_ref[...], (((1,), (1,)), ((), ())), preferred_element_type=F32)
        dh_ref[...] = d_h.astype(BF16).astype(F32)

    @pl.when(step == last)
    def _():
        dh_ref[...] = jnp.zeros_like(dh_ref)


def back_pass(a, b, norm, slope, h, w_t, gamma, core, chunk, old):
    width = norm.shape[1]
    steps = MAIN // BACK
    strip = pl.BlockSpec((BACK, width), lambda i, m: (jnp.minimum(i, steps - 1), 0))
    flat = lambda start, count: pl.BlockSpec((width // 2, BACK), lambda i, m: (0, jnp.clip(i - start, 0, count - 1)))
    at_a, at_b = flat(0, CUT // BACK), flat(CUT // BACK, (MAIN - CUT) // BACK)
    return pl.pallas_call(
        back_body,
        out_shape=(jax.ShapeDtypeStruct(old.shape, F32), jax.ShapeDtypeStruct((width + 32, width), F32)),
        grid_spec=pltpu.PrefetchScalarGridSpec(
            num_scalar_prefetch=1, grid=(steps + 1,),
            in_specs=[
                at_a, at_a, at_b, at_b, strip, strip,
                pl.BlockSpec((BACK, width), lambda i, m: (m[1] * steps + jnp.minimum(i, steps - 1), 0)),
                whole(width, width), whole(1, width), pl.BlockSpec(memory_space=pl.ANY),
            ],
            out_specs=(pl.BlockSpec((BACK, width), lambda i, m: (m[1] * steps + i, 0)), whole(width + 32, width)),
        ),
        input_output_aliases={10: 0},
        compiler_params=params(),
        cost_estimate=pl.CostEstimate(flops=4 * MAIN * width * width, bytes_accessed=MAIN * width * 18, transcendentals=0),
    )(jnp.stack([core, chunk]), *a, *b, norm, slope, h, w_t, gamma, old)


def scatter_body(per, meta_ref, idx_ref, dh_ref, out_ref):
    step = pl.program_id(0)
    seq_len = out_ref.shape[1]
    spot = lax.broadcasted_iota(jnp.int32, (seq_len, WIN), 0).astype(F32)
    for i in range(per):
        hot = (spot == idx_ref[i]).astype(F32).astype(BF16)
        base = pl.multiple_of(meta_ref[step * per + i], 8)
        rows = dh_ref[pl.ds(base, WIN), :].astype(BF16)
        out_ref[i] = jnp.dot(hot, rows, preferred_element_type=F32).astype(BF16)


def scatter_pass(dh, idx_win, base, batch, seq_len):
    width = dh.shape[1]
    per = 4
    return pl.pallas_call(
        functools.partial(scatter_body, per),
        out_shape=jax.ShapeDtypeStruct((batch, seq_len, width), BF16),
        grid_spec=pltpu.PrefetchScalarGridSpec(
            num_scalar_prefetch=1, grid=(batch // per,),
            in_specs=[
                pl.BlockSpec((per, 1, WIN), lambda b, m: (b, 0, 0)),
                whole(*dh.shape),
            ],
            out_specs=pl.BlockSpec((per, seq_len, width), lambda b, m: (b, 0, 0)),
        ),
        compiler_params=pltpu.CompilerParams(dimension_semantics=("arbitrary",), vmem_limit_bytes=VMEM_LIMIT),
        cost_estimate=pl.CostEstimate(flops=2 * batch * WIN * seq_len * width, bytes_accessed=batch * seq_len * width * 2, transcendentals=0),
    )(base, idx_win, dh)


def params():
    return pltpu.CompilerParams(dimension_semantics=("arbitrary",), vmem_limit_bytes=VMEM_LIMIT)


def scratch_array(*shape):
    return pl.pallas_call(
        lambda out_ref: None, out_shape=jax.ShapeDtypeStruct(shape, F32), out_specs=pl.BlockSpec(memory_space=pl.ANY)
    )()


def by_tile(rows, cols, start=0):
    return pl.BlockSpec((rows, cols), lambda j, *_: (j + start, 0))


def strip_of(start=0):
    return pl.BlockSpec((1, VT), lambda j, *_: (0, j + start))


def clear_tail(e_ref, shard):
    tail = shard % VT

    @pl.when(pl.program_id(0) == shard // VT)
    def _():
        e_ref[tail:] = jnp.zeros((VT - tail, e_ref.shape[1]), BF16)


def columns():
    return [slice(i, i + CB) for i in range(0, MAIN, CB)]


def logits_body(shard, target, e_ref, t_ref, bias_ref, lab_ref, soft_ref, stat_ref):
    clear_tail(e_ref, shard)
    bias = jnp.broadcast_to(bias_ref[...], (128, VT)).T
    bias = jnp.concatenate([bias] * (CB // 128), axis=1)
    vocab = lax.broadcasted_iota(jnp.int32, (VT, CB), 0)
    for cols in columns():
        z = jnp.dot(e_ref[...], t_ref[:, cols], preferred_element_type=F32) + bias
        top = jnp.max(z, axis=0, keepdims=True)
        soft = jnp.exp(z - top)
        soft_ref[:, cols] = soft
        stat_ref[FIRST, cols] = top
        stat_ref[SECOND, cols] = jnp.sum(soft, axis=0, keepdims=True)
        if target:
            hot = vocab == lab_ref[:, cols] - pl.program_id(0) * VT
            stat_ref[THIRD, cols] = jnp.sum(jnp.where(hot, z, 0.0), axis=0, keepdims=True)


def logits_pass(embed, t_t, bias, lab, target):
    shard, width = embed.shape
    steps = pl.cdiv(shard, VT)
    return pl.pallas_call(
        functools.partial(logits_body, shard, target),
        out_shape=(jax.ShapeDtypeStruct((steps * VT, MAIN), F32), jax.ShapeDtypeStruct((steps * 8, MAIN), F32)),
        grid_spec=pltpu.PrefetchScalarGridSpec(
            num_scalar_prefetch=0, grid=(steps,),
            in_specs=[by_tile(VT, width), whole(width, MAIN), strip_of(), whole(1, MAIN)],
            out_specs=(by_tile(VT, MAIN), by_tile(8, MAIN)),
        ),
        compiler_params=params(),
        cost_estimate=pl.CostEstimate(flops=2 * MAIN * shard * width, bytes_accessed=MAIN * shard * 4, transcendentals=MAIN * shard),
    )(embed, t_t, bias, lab)


def grad_logits(soft_ref, vec_ref, lab_ref, cols, vocab, step):
    soft = soft_ref[:, cols] * vec_ref[FIRST, cols]
    return jnp.where(vocab == lab_ref[:, cols] - step * VT, soft - vec_ref[SECOND, cols], soft)


def lane_groups(dz):
    acc = dz[:, :128]
    for k in range(128, CB, 128):
        acc = acc + dz[:, k:k + 128]
    return acc


def hidden_body(shard, core_ref, soft_ref, vec_ref, lab_ref, e_ref, dz_ref, keep_ref, give_ref, db_ref, dt_s):
    step = pl.program_id(0)
    half = keep_ref.shape[0]

    @pl.when(step == 0)
    def _():
        dt_s[...] = jnp.zeros_like(dt_s)

    clear_tail(e_ref, shard)
    vocab = lax.broadcasted_iota(jnp.int32, (VT, CB), 0)
    acc = []
    for cols in columns():
        dz = grad_logits(soft_ref, vec_ref, lab_ref, cols, vocab, step)
        acc.append(lane_groups(dz))
        dz = dz.astype(BF16)
        dz_ref[:, cols] = dz
        dt_s[:, cols] += lax.dot_general(e_ref[...], dz, (((0,), (0,)), ((), ())), preferred_element_type=F32)
    db_ref[...] = jnp.sum(sum(acc[1:], acc[0]).T, axis=0, keepdims=True)

    @pl.when(step == pl.num_programs(0) - 1)
    def _():
        core = core_ref[0]
        keep_ref[...] = dt_s[pl.ds(pl.multiple_of(core * half, 8), half), :]
        give_ref[...] = dt_s[pl.ds(pl.multiple_of((1 - core) * half, 8), half), :]


def hidden_pass(soft, vec, lab, embed, core):
    shard, width = embed.shape
    padded = soft.shape[0]
    flat = whole(width // 2, MAIN)
    return pl.pallas_call(
        functools.partial(hidden_body, shard),
        out_shape=(
            jax.ShapeDtypeStruct((padded, MAIN), BF16),
            jax.ShapeDtypeStruct((width // 2, MAIN), F32), jax.ShapeDtypeStruct((width // 2, MAIN), F32),
            jax.ShapeDtypeStruct((1, padded), F32),
        ),
        grid_spec=pltpu.PrefetchScalarGridSpec(
            num_scalar_prefetch=1, grid=(padded // VT,),
            in_specs=[by_tile(VT, MAIN), by_tile(8, MAIN), whole(1, MAIN), by_tile(VT, width)],
            out_specs=(by_tile(VT, MAIN), flat, flat, strip_of()),
            scratch_shapes=[pltpu.VMEM((width, MAIN), F32)],
        ),
        compiler_params=params(),
        cost_estimate=pl.CostEstimate(flops=2 * MAIN * shard * width, bytes_accessed=MAIN * shard * 6, transcendentals=0),
    )(core.reshape(1), soft, vec, lab, embed)


def embed_body(start, meta_ref, dz_ref, soft_ref, vec_ref, lab_ref, t_own_ref, t_oth_ref, db_own_ref, old_ref, de_ref, db_ref, dz_s):
    step = pl.program_id(0) + start
    vocab = lax.broadcasted_iota(jnp.int32, (VT, CB), 0)
    acc = []
    for cols in columns():
        dz = grad_logits(soft_ref, vec_ref, lab_ref, cols, vocab, step)
        acc.append(lane_groups(dz))
        dz_s[:, cols] = dz.astype(BF16)
    old = jnp.where(meta_ref[0] == 0, 0.0, old_ref[...])
    de_ref[...] = old + jnp.dot(dz_ref[...], t_own_ref[...], preferred_element_type=F32)
    de_ref[...] += jnp.dot(dz_s[...], t_oth_ref[...], preferred_element_type=F32)
    db_ref[...] = db_own_ref[...] + jnp.sum(sum(acc[1:], acc[0]).T, axis=0, keepdims=True)


def embed_pass(start, count, dz_own, soft_oth, vec, lab, t_own, t_oth, db_own, old, chunk):
    shard, width = old.shape
    return pl.pallas_call(
        functools.partial(embed_body, start),
        out_shape=(jax.ShapeDtypeStruct((shard, width), F32), jax.ShapeDtypeStruct((1, count * VT), F32)),
        grid_spec=pltpu.PrefetchScalarGridSpec(
            num_scalar_prefetch=1, grid=(count,),
            in_specs=[
                by_tile(VT, MAIN, start), by_tile(VT, MAIN, start), by_tile(8, MAIN, start), whole(1, MAIN),
                whole(MAIN, width), whole(MAIN, width), strip_of(start), by_tile(VT, width, start),
            ],
            out_specs=(by_tile(VT, width, start), strip_of()),
            scratch_shapes=[pltpu.VMEM((VT, MAIN), BF16)],
        ),
        input_output_aliases={8: 0},
        compiler_params=params(),
        cost_estimate=pl.CostEstimate(flops=4 * MAIN * count * VT * width, bytes_accessed=MAIN * count * VT * 6 + count * VT * width * 4, transcendentals=0),
    )(chunk.reshape(1), dz_own, soft_oth, vec, lab, t_own, t_oth, db_own, old)


def combine(stat):
    top, tot, hit = (stat.reshape(-1, 8, MAIN)[:, i] for i in range(3))
    best = jnp.max(top, axis=0)
    stats = jnp.stack([best, jnp.sum(tot * jnp.exp(top - best), axis=0), jnp.sum(hit, axis=0)])
    for swap in (swap_core, swap_x):
        other = swap(stats)
        best = jnp.maximum(stats[0], other[0])
        stats = jnp.stack([
            best,
            stats[1] * jnp.exp(stats[0] - best) + other[1] * jnp.exp(other[0] - best),
            stats[2] + other[2],
        ])
    return stats, top


def tie(*values):
    return lax.optimization_barrier(values)


def solution(mesh):
    def local_step(hidden, positions, labels, weights, w_t, b_t, gamma, beta, embed, out_bias):
        batch, seq_len, width = hidden.shape
        max_pred = positions.shape[1]
        shard_vocab = embed.shape[0]
        tiles = pl.cdiv(shard_vocab, VT)
        tp = lax.axis_index("tp")
        core = tp % 2
        counts = jnp.sum(weights, axis=1).astype(jnp.int32)
        seq = jnp.arange(batch, dtype=jnp.int32)
        offsets = jnp.sum(jnp.where(seq[None, :] < seq[:, None], counts[None, :], 0), 1)
        n_own = jnp.sum(counts)
        n_oth = swap_dp(jnp.full((8, 128), n_own, jnp.int32))
        shift = offsets % 8
        base = offsets - shift
        live = jnp.where(jnp.arange(max_pred)[None, :] < counts[:, None], positions, -1).astype(F32)
        idx_win = jnp.full((batch, WIN), -1.0, F32)
        for k in range(8):
            moved = jnp.pad(live, ((0, 0), (k, WIN - max_pred - k)), constant_values=-1.0)
            idx_win = jnp.where((shift == k)[:, None], moved, idx_win)
        idx_win = idx_win[:, None, :]
        tok_rows = gather_pass(hidden, idx_win, base, CHUNKS * MAIN)
        n_oth, tok_rows = tie(n_oth, tok_rows)
        n_oth = n_oth[0, 0]
        trips = jnp.where(jnp.maximum(n_own, n_oth) > MAIN, CHUNKS, 1)
        denom = (n_own + n_oth).astype(F32) + LOSS_EPS
        bias = jnp.pad(out_bias, (0, tiles * VT - shard_vocab), constant_values=-jnp.inf)[None, :]
        vecs = jnp.stack([b_t, gamma, beta] + [jnp.zeros_like(b_t)] * 5)

        def local_labels(lab):
            lab = lab - tp * shard_vocab
            return jnp.where((lab >= 0) & (lab < shard_vocab), lab, -1)[None, :]

        def trip(carry):
            chunk, d_embed, d_rows, pack_sum, bias_sum, loss_sum = carry
            row = chunk * MAIN + jnp.arange(MAIN, dtype=jnp.int32)
            in_seq = (row[:, None] >= offsets[None, :]) & (row[:, None] < (offsets + counts)[None, :])
            slot_row = jnp.where(row < n_own, row - jnp.sum(jnp.where(in_seq, offsets[None, :], 0), 1), -1)
            lab_seq = jnp.dot(in_seq.astype(F32), labels.astype(F32), precision=lax.Precision.HIGHEST)
            slot_hot = slot_row[:, None] == jnp.arange(max_pred, dtype=jnp.int32)[None, :]
            lab_own = jnp.sum(jnp.where(slot_hot, lab_seq, 0.0), 1).astype(jnp.int32)
            lab_oth = swap_dp(lab_own)

            def vectors(stats, tops, n):
                scale = (row < n).astype(F32) / denom
                factor = jnp.exp(tops - stats[0]) * (scale / stats[1])
                first = jnp.arange(8, dtype=jnp.int32)[:, None] == 0
                return jnp.where(first, factor[:, None], scale).reshape(-1, MAIN)

            t_own, t_own_t, norm, slope, send = transform_pass(tok_rows, w_t, vecs, tp, chunk)
            got = swap_dp(send)
            soft_own, stat_own = logits_pass(embed, t_own_t, bias, local_labels(lab_own), True)
            got, stat_own, lab_oth = tie(got, stat_own, lab_oth)
            stat_own, tops_own = combine(stat_own)
            got_x, got_core = swap_x(got), swap_core(got)
            loss_sum = loss_sum + jnp.sum(jnp.where(row < n_own, jnp.log(stat_own[1]) + stat_own[0] - stat_own[2], 0.0))
            dz_own, keep, give, db_own = hidden_pass(soft_own, vectors(stat_own, tops_own, n_own), local_labels(lab_own), embed, core)
            got_x, got_core, keep = tie(got_x, got_core, keep)
            got_far = swap_core(got_x)
            given = swap_core(give)
            t_oth, t_oth_t = collect_pass((got, got_x, got_core, got_far), tp)
            given, t_oth_t = tie(given, t_oth_t)
            chip_a, chip_b = keep[:, :CUT] + given[:, :CUT], keep[:, CUT:] + given[:, CUT:]
            chip_a, chip_b, t_oth_t = tie(chip_a, chip_b, t_oth_t)
            other_a = swap_x(chip_a)
            soft_oth, stat_oth = logits_pass(embed, t_oth_t, bias, local_labels(lab_oth), False)
            other_a, stat_oth = tie(other_a, stat_oth)
            stat_oth, tops_oth = combine(stat_oth)
            chip_b, stat_oth = tie(chip_b, stat_oth)
            other_b = swap_x(chip_b)
            mine_a = chip_a + other_a
            theirs_a = swap_core(mine_a)
            vec_oth = vectors(stat_oth, tops_oth, n_oth)

            def embed_tiles(start, count, old):
                return embed_pass(start, count, dz_own, soft_oth, vec_oth, local_labels(lab_oth), t_own, t_oth, db_own, old, chunk)

            d_embed, db_0 = embed_tiles(0, 7, d_embed)
            other_b, theirs_a, d_embed = tie(other_b, theirs_a, d_embed)
            mine_b = chip_b + other_b
            theirs_b = swap_core(mine_b)
            d_rows, pack = back_pass((mine_a, theirs_a), (mine_b, theirs_b), norm, slope, tok_rows, w_t, gamma[None, :], core, chunk, d_rows)
            quarter = pack.shape[0] // 4
            pack = lax.dynamic_slice_in_dim(pack, tp * quarter, quarter)
            pack, d_embed = tie(pack, d_embed)
            far = swap_dp(pack)
            d_embed, db_1 = embed_tiles(7, tiles - 7, d_embed)
            far, d_embed = tie(far, d_embed)
            bias_sum = bias_sum + jnp.concatenate([db_0, db_1], axis=1)
            return chunk + 1, d_embed, d_rows, pack_sum + (pack + far), bias_sum, loss_sum

        start = (
            jnp.int32(0), scratch_array(shard_vocab, width), scratch_array(CHUNKS * MAIN + BACK, width),
            jnp.zeros(((width + 32) // 4, width), F32), jnp.zeros((1, tiles * VT), F32), jnp.zeros((), F32),
        )
        _, d_embed, d_rows, pack, d_out_bias, loss = lax.while_loop(lambda carry: carry[0] < trips, trip, start)
        far = swap_x(pack)
        loss_oth = swap_dp(jnp.full((8, 128), loss))
        d_hidden = scatter_pass(d_rows, idx_win, base, batch, seq_len)
        far, loss_oth, d_hidden = tie(far, loss_oth, d_hidden)
        pair = jnp.where(tp // 2 == 0, jnp.stack([pack, far]), jnp.stack([far, pack]))
        theirs = swap_core(pair)
        pack = jnp.where(core == 0, jnp.stack([pair, theirs], 1), jnp.stack([theirs, pair], 1)).reshape(-1, width)
        loss = (loss + loss_oth[0, 0]) / denom
        return loss, d_hidden, pack[:width], pack[width], pack[width + 1], pack[width + 2], d_embed, d_out_bias[0, :shard_vocab]

    in_specs = (P("dp", None, None), P("dp", None), P("dp", None), P("dp", None), P(None, None), P(None), P(None), P(None), P("tp", None), P("tp"))
    out_specs = (P(), P("dp", None, None), P(None, None), P(None), P(None), P(None), P("tp", None), P("tp"))
    return jax.shard_map(local_step, mesh=mesh, in_specs=in_specs, out_specs=out_specs, check_vma=False)
```

profile of v0, /device:TPU:0, one launch (start us, length us, event | category | flops | bytes accessed | tf_op | source)
XLA Modules:
  0.0 313.8 jit_solution(4032973738767233826)
XLA Ops:
  0.6 0.8 reduce_sum.111
  1.6 1.1 add_bitcast_fusion
  3.4 3.4 %collective-permute-start.15 = (s32[8,128]{1,0:T(8,128)S(1)}, s32[8,128]{1,0:T(8,128)S(1)}, u32[]{:S(2)}, u32[]{:S(2)}) collective-permute-start(s32[8,128]{1,0:T(8,128)S(1)} %broadcast_in_dim.211), channel_id=1, source_target_pairs={{0,4},{4,0},{1,5},{5,1},{2,6},{6,2},{3,7},{7,3}} | collective-permute-start | bytes 12296 | tf_op jit(solution)/shard_map/ppermute | solution.py:35
  6.8 0.8 select_convert_fusion
  7.6 0.7 select_select_fusion
  8.3 15.7 %shard_map.172 = bf16[3072,768]{1,0:T(8,128)(2,1)} custom-call(s32[32]{0:T(128)} %get-tuple-element.645.meta_ref, f32[32,1,128]{2,1,0:T(1,128)} %bitcast.100, bf16[32,512,768]{2,1,0:T(8,128)(2,1)} %h_ref.1), custom_call_target="tpu_custom_call" | custom-call | flops 3221225472 | bytes 25165824 | tf_op jit(solution)/shard_map/pallas_call | solution.py:70
  28.0 0.9 broadcast_in_dim.209
  28.9 259.7 %while.23 = (s32[]{:T(128)}, f32[7648,768]{1,0:T(8,128)}, f32[3328,768]{1,0:T(8,128)}, f32[200,768]{1,0:T(8,128)}, f32[1,7680]{1,0:T(1,128)S(1)}, /*index=5*/f32...) while((s32[]{:T(128)}, f32[7648,768]{1,0:T(8,128)}, ...), condition=%wide.wide.region_13.14_spmd.clone, body=%wide.wide.region_3.13_spmd.sunk.clone.sunk | while | flops 95857770496 | bytes 422334880 | solution.py:521
  31.1 14.1 %body.32 = (bf16[1536,768]{1,0:T(8,128)(2,1)}, bf16[768,1536]{1,0:T(8,128)(2,1)}, f32[1536,768]{1,0:T(8,128)}, f32[1536,768]{1,0:T(8,128)}, f32[384,768]{1,0:T(8,128)}) custom-call(s32[2]{0:T(128)} %pad_add_fusion.7.meta_ref, bf16[3072,768]{1,0:T(8,128)(2,1)} %get-tuple-element.1165.h_ref, bf16[768,768]{1,0:T(8,128)(2,1)} %get-tuple-element.1166.w_ref, ...), custom_call_target="tpu_custom_call" | custom-call | flops 1811939328 | bytes 16515072 | tf_op jit(solution)/shard_map/while/body/pallas_call | solution.py:118
  45.3 2.0 collective-permute-start
  47.8 34.6 %body.33 = (f32[7680,1536]{1,0:T(8,128)}, f32[120,1536]{1,0:T(8,128)}) custom-call(bf16[7648,768]{1,0:T(8,128)(2,1)} %get-tuple-element.1173.e_ref, bf16[768,1536]{1,0:T(8,128)(2,1)} %get-tuple-element.1032.t_ref, f32[1,7680]{1,0:T(1,128)S(1)} %get-tuple-element.1174.bias_ref, s32[1,1536]{1,0:T(1,128)} %and_select_fusion.8.lab_ref), custom_call_target="tpu_custom_call" | custom-call | flops 18043895808 | bytes 46989312 | tf_op jit(solution)/shard_map/while/body/pallas_call | solution.py:300
  82.5 2.1 slice_reduce_fusion.25
  86.0 1.5 collective-permute-start.3
  88.1 1.7 collective-permute-done.3
  89.8 0.7 slice_reduce_fusion.27
  90.6 1.0 bitcast_select_fusion.6.vec_ref
  91.6 39.4 %body.34 = (bf16[7680,1536]{1,0:T(8,128)(2,1)}, f32[384,1536]{1,0:T(8,128)}, f32[384,1536]{1,0:T(8,128)}, f32[1,7680]{1,0:T(1,128)}) custom-call(s32[1]{0:T(128)} %bitcast.85.core_ref, f32[7680,1536]{1,0:T(8,128)} %get-tuple-element.1033.soft_ref, f32[120,1536]{1,0:T(8,128)} %bitcast_select_fusion.6.vec_ref, s32[1,1536]{1,0:T(1,128)} %and_select_fusion.8.lab_ref, ...), custom_call_target="tpu_custom_call" | custom-call | flops 18043895808 | bytes 70483968 | tf_op jit(solution)/shard_map/while/body/pallas_call | solution.py:355
  132.7 4.5 %collective-permute-done.7.refs_3_ = f32[384,768]{1,0:T(8,128)} collective-permute-done((f32[384,768]{1,0:T(8,128)S(1)}, f32[384,768]{1,0:T(8,128)}, u32[]{:S(2)}, u32[]{:S(2)}) %collective-permute-start.7) | collective-permute-done | bytes 1179680 | tf_op jit(solution)/shard_map/while/body/ppermute | solution.py:39
  137.2 6.1 %body.35 = (bf16[1536,768]{1,0:T(8,128)(2,1)}, bf16[768,1536]{1,0:T(8,128)(2,1)}) custom-call(s32[4]{0:T(128)} %broadcast_xor_fusion.3.place_ref, f32[384,768]{1,0:T(8,128)} %collective-permute-done.refs_0_, f32[384,768]{1,0:T(8,128)} %copy-done.8, f32[384,768]{1,0:T(8,128)} %collective-permute-done.6.refs_2_, f32[384,768]{1,0:T(8,128)} %collective-permute-done.7.refs_3_), custom_call_target="tpu_custom_call" | custom-call | flops 1179648 | bytes 9437184 | tf_op jit(solution)/shard_map/while/body/pallas_call | solution.py:148
  143.3 2.3 slice_add_fusion.10
  145.9 1.9 collective-permute-start.8
  147.8 32.0 %body.36 = (f32[7680,1536]{1,0:T(8,128)}, f32[120,1536]{1,0:T(8,128)}) custom-call(bf16[7648,768]{1,0:T(8,128)(2,1)} %get-tuple-element.1173.e_ref, bf16[768,1536]{1,0:T(8,128)(2,1)} %get-tuple-element.1056.t_ref, f32[1,7680]{1,0:T(1,128)S(1)} %get-tuple-element.1174.bias_ref, s32[1,1536]{1,0:T(1,128)} %broadcast_in_dim.327.lab_ref), custom_call_target="tpu_custom_call" | custom-call | flops 18043895808 | bytes 46989312 | tf_op jit(solution)/shard_map/while/body/pallas_call | solution.py:300
  179.9 2.7 collective-permute-done.8
  182.5 2.4 slice_reduce_fusion.28
  185.1 1.2 collective-permute-done.9
  186.3 1.8 collective-permute-start.10
  188.7 1.8 add.463.mine_a_ref
  190.6 0.7 slice_reduce_fusion.29
  191.3 1.4 collective-permute-start.11
  192.7 1.0 bitcast_select_fusion.7.vec_ref
  193.7 26.3 %body.37 = (f32[7648,768]{1,0:T(8,128)}, f32[1,3584]{1,0:T(1,128)}) custom-call(s32[1]{0:T(128)} %bitcast.86.meta_ref, bf16[7680,1536]{1,0:T(8,128)(2,1)} %get-tuple-element.1073.dz_ref, f32[7680,1536]{1,0:T(8,128)} %get-tuple-element.1074.soft_ref, f32[120,1536]{1,0:T(8,128)} %bitcast_select_fusion.7.vec_ref, ...), custom_call_target="tpu_custom_call", output_to_operand_aliasing={{0}: (8, {})} | custom-call | flops 16911433728 | bytes 44040192 | tf_op jit(solution)/shard_map/while/body/pallas_call | solution.py:389
  220.0 1.1 copy-done.3
  221.2 1.3 add.464.mine_b_ref
  222.5 0.7 pad_add_fusion.6.meta_ref
  223.2 1.3 select_reduce_fusion.8
  225.1 0.9 copy-done.9
  225.9 15.1 %body.38 = (f32[3328,768]{1,0:T(8,128)}, f32[800,768]{1,0:T(8,128)}) custom-call(s32[2]{0:T(128)} %pad_add_fusion.6.meta_ref, f32[384,1024]{1,0:T(8,128)} %copy-done, f32[384,1024]{1,0:T(8,128)} %copy-done.3, f32[384,512]{1,0:T(8,128)} %copy-done.1, f32[384,512]{1,0:T(8,128)} %copy-done.9, ...), custom_call_target="tpu_custom_call", output_to_operand_aliasing={{0}: (10, {})} | custom-call | flops 3623878656 | bytes 21233664 | tf_op jit(solution)/shard_map/while/body/pallas_call | solution.py:202
  241.0 1.1 constant_dynamic-slice_fusion.3
  242.2 29.2 %body.39 = (f32[7648,768]{1,0:T(8,128)}, f32[1,4096]{1,0:T(1,128)}) custom-call(s32[1]{0:T(128)} %bitcast.86.meta_ref, bf16[7680,1536]{1,0:T(8,128)(2,1)} %get-tuple-element.1073.dz_ref, f32[7680,1536]{1,0:T(8,128)} %get-tuple-element.1074.soft_ref, f32[120,1536]{1,0:T(8,128)} %bitcast_select_fusion.7.vec_ref, ...), custom_call_target="tpu_custom_call", output_to_operand_aliasing={{0}: (8, {})} | custom-call | flops 19327352832 | bytes 50331648 | tf_op jit(solution)/shard_map/while/body/pallas_call | solution.py:389
  272.0 0.8 maximum_add_fusion.3
  272.8 14.8 %collective-permute-done.14 = f32[200,768]{1,0:T(8,128)S(1)} collective-permute-done((f32[200,768]{1,0:T(8,128)S(1)}, f32[200,768]{1,0:T(8,128)S(1)}, u32[]{:S(2)}, u32[]{:S(2)}) %collective-permute-start.14) | collective-permute-done | bytes 614432 | tf_op jit(solution)/shard_map/while/body/ppermute | solution.py:35
  287.8 0.8 copy-done.5
  288.7 0.7 collective-permute-start.16
  289.9 16.3 %shard_map.173 = bf16[32,512,768]{2,1,0:T(8,128)(2,1)} custom-call(s32[32]{0:T(128)} %get-tuple-element.645.meta_ref, f32[32,1,128]{2,1,0:T(1,128)} %bitcast.101, f32[3328,768]{1,0:T(8,128)} %get-tuple-element.1216), custom_call_target="tpu_custom_call" | custom-call | flops 3221225472 | bytes 25165824 | tf_op jit(solution)/shard_map/pallas_call | solution.py:234
  306.3 1.1 maximum_select_fusion.2
  307.4 0.7 slice_reduce_fusion.11
  309.4 0.9 collective-permute-done.18
  310.5 1.6 slice.246
  (118 shorter events, 12.4 us)
Async XLA Ops:
  3.4 21.5 %collective-permute-start.15 = (s32[8,128]{1,0:T(8,128)S(1)}, s32[8,128]{1,0:T(8,128)S(1)}, u32[]{:S(2)}, u32[]{:S(2)}) collective-permute-start(s32[8,128]{1,0:T(8,128)S(1)} %broadcast_in_dim.211), channel_id=1, source_target_pairs={{0,4},{4,0},{1,5},{5,1},{2,6},{6,2},{3,7},{7,3}} | collective-permute-start | bytes 12296 | tf_op jit(solution)/shard_map/ppermute | solution.py:35
  24.0 0.7 copy-start.12
  24.0 0.7 copy-start.14
  24.0 0.7 copy-start.15
  24.0 0.8 copy-start.11
  24.0 0.8 copy-start.13
  24.0 4.9 %copy-start.16 = (s32[4]{0:T(128)S(1)}, s32[4]{0:T(128)}, u32[]{:S(2)}) copy-start(s32[4]{0:T(128)} %constant.137.clone..sunk.3) | copy-start | bytes 52
  30.4 52.0 %collective-permute-start.1 = (s32[1536]{0:T(1024)S(1)}, s32[1536]{0:T(1024)S(1)}, u32[]{:S(2)}, u32[]{:S(2)}) collective-permute-start(s32[1536]{0:T(1024)S(1)} %convert_element_type.63), channel_id=1, source_target_pairs={{0,4},{4,0},{1,5},{5,1},{2,6},{6,2},{3,7},{7,3}} | collective-permute-start | bytes 18440 | tf_op jit(solution)/shard_map/while/body/ppermute | solution.py:35
  45.3 37.2 %collective-permute-start = (f32[384,768]{1,0:T(8,128)}, f32[384,768]{1,0:T(8,128)}, u32[]{:S(2)}, u32[]{:S(2)}) collective-permute-start(f32[384,768]{1,0:T(8,128)} %get-tuple-element.1034), channel_id=1, source_target_pairs={{0,4},{4,0},{1,5},{5,1},{2,6},{6,2},{3,7},{7,3}} | collective-permute-start | bytes 3538952 | tf_op jit(solution)/shard_map/while/body/ppermute | solution.py:35
  84.6 1.2 collective-permute-start.2
  86.0 3.8 %collective-permute-start.3 = (f32[3,1536]{1,0:T(4,128)S(1)}, f32[3,1536]{1,0:T(4,128)S(1)}, u32[]{:S(2)}, u32[]{:S(2)}) collective-permute-start(f32[3,1536]{1,0:T(4,128)S(1)} %pad_maximum_fusion.16), channel_id=1, source_target_pairs={{0,2},{1,3},{2,0},{3,1},{4,6},{5,7},{6,4},{7,5}} | collective-permute-start | bytes 55304 | tf_op jit(solution)/shard_map/while/body/ppermute | solution.py:43
  87.6 43.5 %collective-permute-start.5 = (f32[384,768]{1,0:T(8,128)}, f32[384,768]{1,0:T(8,128)S(1)}, u32[]{:S(2)}, u32[]{:S(2)}) collective-permute-start(f32[384,768]{1,0:T(8,128)} %collective-permute-done.refs_0_), channel_id=1, source_target_pairs={{0,2},{1,3},{2,0},{3,1},{4,6},{5,7},{6,4},{7,5}} | collective-permute-start | bytes 3538952 | tf_op jit(solution)/shard_map/while/body/ppermute | solution.py:43
  88.1 43.0 %collective-permute-start.6 = (f32[384,768]{1,0:T(8,128)}, f32[384,768]{1,0:T(8,128)}, u32[]{:S(2)}, u32[]{:S(2)}) collective-permute-start(f32[384,768]{1,0:T(8,128)} %collective-permute-done.refs_0_), channel_id=1, source_target_pairs={{0,1},{1,0},{2,3},{3,2},{4,5},{5,4},{6,7},{7,6}} | collective-permute-start | bytes 3538952 | tf_op jit(solution)/shard_map/while/body/ppermute | solution.py:39
  131.0 12.3 %collective-permute-start.4 = (f32[384,1536]{1,0:T(8,128)}, f32[384,1536]{1,0:T(8,128)S(1)}, u32[]{:S(2)}, u32[]{:S(2)}) collective-permute-start(f32[384,1536]{1,0:T(8,128)} %get-tuple-element.1046), channel_id=1, source_target_pairs={{0,1},{1,0},{2,3},{3,2},{4,5},{5,4},{6,7},{7,6}} | collective-permute-start | bytes 7077896 | tf_op jit(solution)/shard_map/while/body/ppermute | solution.py:39
  131.1 6.1 %copy-start.8 = (f32[384,768]{1,0:T(8,128)}, f32[384,768]{1,0:T(8,128)S(1)}, u32[]{:S(2)}) copy-start(f32[384,768]{1,0:T(8,128)S(1)} %collective-permute-done.5.refs_1_) | copy-start | bytes 3538948 | tf_op jit(solution)/shard_map/while
  131.1 6.1 %collective-permute-start.7 = (f32[384,768]{1,0:T(8,128)S(1)}, f32[384,768]{1,0:T(8,128)}, u32[]{:S(2)}, u32[]{:S(2)}) collective-permute-start(f32[384,768]{1,0:T(8,128)S(1)} %collective-permute-done.5.refs_1_), channel_id=1, source_target_pairs={{0,1},{1,0},{2,3},{3,2},{4,5},{5,4},{6,7},{7,6}} | collective-permute-start | bytes 3538952 | tf_op jit(solution)/shard_map/while/body/ppermute | solution.py:39
  143.3 2.4 copy-start.2
  145.9 36.6 %collective-permute-start.8 = (f32[384,1024]{1,0:T(8,128)S(1)}, f32[384,1024]{1,0:T(8,128)S(1)}, u32[]{:S(2)}, u32[]{:S(2)}) collective-permute-start(f32[384,1024]{1,0:T(8,128)S(1)} %slice_add_fusion.9), channel_id=1, source_target_pairs={{0,2},{1,3},{2,0},{3,1},{4,6},{5,7},{6,4},{7,5}} | collective-permute-start | bytes 4718600 | tf_op jit(solution)/shard_map/while/body/ppermute | solution.py:43
  182.5 5.5 %copy-start.7 = (f32[384,1024]{1,0:T(8,128)}, f32[384,1024]{1,0:T(8,128)S(1)}, u32[]{:S(2)}) copy-start(f32[384,1024]{1,0:T(8,128)S(1)} %collective-permute-done.8) | copy-start | bytes 4718596 | tf_op jit(solution)/shard_map/while
  185.0 1.2 collective-permute-start.9
  186.3 4.2 %collective-permute-start.10 = (f32[3,1536]{1,0:T(4,128)S(1)}, f32[3,1536]{1,0:T(4,128)S(1)}, u32[]{:S(2)}, u32[]{:S(2)}) collective-permute-start(f32[3,1536]{1,0:T(4,128)S(1)} %pad_maximum_fusion.18), channel_id=1, source_target_pairs={{0,2},{1,3},{2,0},{3,1},{4,6},{5,7},{6,4},{7,5}} | collective-permute-start | bytes 55304 | tf_op jit(solution)/shard_map/while/body/ppermute | solution.py:43
  190.5 29.5 %copy-start = (f32[384,1024]{1,0:T(8,128)}, f32[384,1024]{1,0:T(8,128)S(1)}, u32[]{:S(2)}) copy-start(f32[384,1024]{1,0:T(8,128)S(1)} %add.463.mine_a_ref) | copy-start | bytes 4718596 | tf_op jit(solution)/shard_map/while
  190.5 29.5 %collective-permute-start.12 = (f32[384,1024]{1,0:T(8,128)S(1)}, f32[384,1024]{1,0:T(8,128)S(1)}, u32[]{:S(2)}, u32[]{:S(2)}) collective-permute-start(f32[384,1024]{1,0:T(8,128)S(1)} %add.463.mine_a_ref), channel_id=1, source_target_pairs={{0,1},{1,0},{2,3},{3,2},{4,5},{5,4},{6,7},{7,6}} | collective-permute-start | bytes 4718600 | tf_op jit(solution)/shard_map/while/body/ppermute | solution.py:39
  191.3 28.7 %collective-permute-start.11 = (f32[384,512]{1,0:T(8,128)}, f32[384,512]{1,0:T(8,128)S(1)}, u32[]{:S(2)}, u32[]{:S(2)}) collective-permute-start(f32[384,512]{1,0:T(8,128)} %slice_add_fusion.10), channel_id=1, source_target_pairs={{0,2},{1,3},{2,0},{3,1},{4,6},{5,7},{6,4},{7,5}} | collective-permute-start | bytes 2359304 | tf_op jit(solution)/shard_map/while/body/ppermute | solution.py:43
  220.0 1.1 copy-start.3
  222.4 2.6 copy-start.1
  222.5 2.6 collective-permute-start.13
  225.0 0.9 copy-start.9
  242.2 29.8 %copy-start.10 = (f32[1,3584]{1,0:T(1,128)S(1)}, f32[1,3584]{1,0:T(1,128)}, u32[]{:S(2)}) copy-start(f32[1,3584]{1,0:T(1,128)} %get-tuple-element.1095) | copy-start | bytes 43012 | tf_op jit(solution)/shard_map/while
  242.2 45.4 %copy-start.4 = (f32[200,768]{1,0:T(8,128)S(1)}, f32[200,768]{1,0:T(8,128)}, u32[]{:S(2)}) copy-start(f32[200,768]{1,0:T(8,128)} %get-tuple-element.1132) | copy-start | bytes 1843204 | tf_op jit(solution)/shard_map/while
  271.4 17.3 %copy-start.17 = (s32[4]{0:T(128)S(1)}, s32[4]{0:T(128)}, u32[]{:S(2)}) copy-start(s32[4]{0:T(128)} %get-tuple-element.1241) | copy-start | bytes 52 | tf_op jit(solution)/shard_map/while
  271.4 16.2 %collective-permute-start.14 = (f32[200,768]{1,0:T(8,128)S(1)}, f32[200,768]{1,0:T(8,128)S(1)}, u32[]{:S(2)}, u32[]{:S(2)}) collective-permute-start(f32[200,768]{1,0:T(8,128)S(1)} %constant_dynamic-slice_fusion.3), channel_id=1, source_target_pairs={{0,4},{4,0},{1,5},{5,1},{2,6},{6,2},{3,7},{7,3}} | collective-permute-start | bytes 1843208 | tf_op jit(solution)/shard_map/while/body/ppermute | solution.py:35
  287.8 0.9 copy-start.5
  288.7 17.6 %collective-permute-start.16 = (f32[200,768]{1,0:T(8,128)}, f32[200,768]{1,0:T(8,128)S(1)}, u32[]{:S(2)}, u32[]{:S(2)}) collective-permute-start(f32[200,768]{1,0:T(8,128)} %get-tuple-element.1217), channel_id=1, source_target_pairs={{0,2},{1,3},{2,0},{3,1},{4,6},{5,7},{6,4},{7,5}} | collective-permute-start | bytes 1843208 | tf_op jit(solution)/shard_map/ppermute | solution.py:43
  289.4 16.9 %collective-permute-start.17 = (f32[8,128]{1,0:T(8,128)S(1)}, f32[8,128]{1,0:T(8,128)S(1)}, u32[]{:S(2)}, u32[]{:S(2)}) collective-permute-start(f32[8,128]{1,0:T(8,128)S(1)} %broadcast_in_dim.226), channel_id=1, source_target_pairs={{0,4},{4,0},{1,5},{5,1},{2,6},{6,2},{3,7},{7,3}} | collective-permute-start | bytes 12296 | tf_op jit(solution)/shard_map/ppermute | solution.py:35
  289.9 16.3 %copy-start.6 = (f32[200,768]{1,0:T(8,128)S(1)}, f32[200,768]{1,0:T(8,128)}, u32[]{:S(2)}) copy-start(f32[200,768]{1,0:T(8,128)} %get-tuple-element.1217) | copy-start | bytes 1843204
  307.4 2.9 collective-permute-start.18
where the time goes:
time: 315 us; the launch traced here: 314 us
  Pallas kernels  229 us (73%)
  waiting for transfers between devices  26.3 us (8%)
  other arithmetic  25.7 us (8%)
  starting transfers between devices  15 us (5%)
  local copies, waits for them, and re-layouts  11 us (3%)
  between operations  5.21 us (2%)
    pallas_call x2, Pallas kernels, logits_pass(): pl.pallas_call(functools.partial(logits_body, shard, target), out_shape=(...  66.7 us
    pallas_call x2, Pallas kernels, embed_pass(): pl.pallas_call(functools.partial(embed_body, start), out_shape=(jax.Shape...  55.5 us
    pallas_call x1, Pallas kernels, hidden_pass(): pl.pallas_call(functools.partial(hidden_body, shard), out_shape=(jax.Shap...  39.4 us
    pallas_call x1, Pallas kernels, scatter_pass(): pl.pallas_call(functools.partial(scatter_body, per), out_shape=jax.ShapeD...  16.3 us
    pallas_call x1, Pallas kernels, gather_pass(): pl.pallas_call(functools.partial(gather_body, per), out_shape=jax.ShapeDt...  15.7 us
    pallas_call x1, Pallas kernels, back_pass(): pl.pallas_call(back_body, out_shape=(jax.ShapeDtypeStruct(old.shape, F32)...  15.1 us
    ppermute x5, waiting for transfers between devices, swap_dp(): return lax.ppermute(x, 'dp', SWAP_DP)  14.8 us
    pallas_call x1, Pallas kernels, transform_pass(): pl.pallas_call(transform_body, out_shape=(jax.ShapeDtypeStruct((MAIN, wid...  14.1 us
  transfers between devices with their start and end apart: 19, of which 7 were waited for; matrix products, arithmetic and copies ran while one was open for 5% of the time, Pallas kernels for 59%

commit v1 on v0

--- a/solution.py
+++ b/solution.py
@@ -6,6 +6,7 @@
 from jax.experimental import pallas as pl
 from jax.experimental.pallas import tpu as pltpu
 from jax.sharding import PartitionSpec as P
+
 
 LN_EPS = 1e-12
 LOSS_EPS = 1e-5
@@ -223,14 +224,15 @@
     spot = lax.broadcasted_iota(jnp.int32, (seq_len, WIN), 0).astype(F32)
     for i in range(per):
         hot = (spot == idx_ref[i]).astype(F32).astype(BF16)
-        base = pl.multiple_of(meta_ref[step * per + i], 8)
-        rows = dh_ref[pl.ds(base, WIN), :].astype(BF16)
+        at = pl.multiple_of((meta_ref[step * per + i] - meta_ref[step * per]) * 8, 8)
+        rows = dh_ref[pl.ds(at, WIN), :].astype(BF16)
         out_ref[i] = jnp.dot(hot, rows, preferred_element_type=F32).astype(BF16)
 
 
-def scatter_pass(dh, idx_win, base, batch, seq_len):
+def scatter_pass(dh, idx_win, base, batch, seq_len, max_pred):
     width = dh.shape[1]
     per = 4
+    span = (per - 1) * max_pred + WIN
     return pl.pallas_call(
         functools.partial(scatter_body, per),
         out_shape=jax.ShapeDtypeStruct((batch, seq_len, width), BF16),
@@ -238,13 +240,13 @@
             num_scalar_prefetch=1, grid=(batch // per,),
             in_specs=[
                 pl.BlockSpec((per, 1, WIN), lambda b, m: (b, 0, 0)),
-                whole(*dh.shape),
+                pl.BlockSpec((pl.Element(span), pl.Element(width)), lambda b, m: (m[b * per] * 8, 0)),
             ],
             out_specs=pl.BlockSpec((per, seq_len, width), lambda b, m: (b, 0, 0)),
         ),
         compiler_params=pltpu.CompilerParams(dimension_semantics=("arbitrary",), vmem_limit_bytes=VMEM_LIMIT),
         cost_estimate=pl.CostEstimate(flops=2 * batch * WIN * seq_len * width, bytes_accessed=batch * seq_len * width * 2, transcendentals=0),
-    )(base, idx_win, dh)
+    )(lax.div(base, 8), idx_win, dh)
 
 
 def params():
@@ -336,9 +338,8 @@
     for cols in columns():
         dz = grad_logits(soft_ref, vec_ref, lab_ref, cols, vocab, step)
         acc.append(lane_groups(dz))
-        dz = dz.astype(BF16)
-        dz_ref[:, cols] = dz
-        dt_s[:, cols] += lax.dot_general(e_ref[...], dz, (((0,), (0,)), ((), ())), preferred_element_type=F32)
+        dz_ref[:, cols] = dz.astype(BF16)
+    dt_s[...] += lax.dot_general(e_ref[...], dz_ref[...], (((0,), (0,)), ((), ())), preferred_element_type=F32)
     db_ref[...] = jnp.sum(sum(acc[1:], acc[0]).T, axis=0, keepdims=True)
 
     @pl.when(step == pl.num_programs(0) - 1)
@@ -481,7 +482,7 @@
             loss_sum = loss_sum + jnp.sum(jnp.where(row < n_own, jnp.log(stat_own[1]) + stat_own[0] - stat_own[2], 0.0))
             dz_own, keep, give, db_own = hidden_pass(soft_own, vectors(stat_own, tops_own, n_own), local_labels(lab_own), embed, core)
             got_x, got_core, keep = tie(got_x, got_core, keep)
-            got_far = swap_core(got_x)
+            got_far, give = tie(swap_core(got_x), give)
             given = swap_core(give)
             t_oth, t_oth_t = collect_pass((got, got_x, got_core, got_far), tp)
             given, t_oth_t = tie(given, t_oth_t)
@@ -521,7 +522,7 @@
         _, d_embed, d_rows, pack, d_out_bias, loss = lax.while_loop(lambda carry: carry[0] < trips, trip, start)
         far = swap_x(pack)
         loss_oth = swap_dp(jnp.full((8, 128), loss))
-        d_hidden = scatter_pass(d_rows, idx_win, base, batch, seq_len)
+        d_hidden = scatter_pass(d_rows, idx_win, base, batch, seq_len, max_pred)
         far, loss_oth, d_hidden = tie(far, loss_oth, d_hidden)
         pair = jnp.where(tp // 2 == 0, jnp.stack([pack, far]), jnp.stack([far, pack]))
         theirs = swap_core(pair)

time: 315 us -> 326 us (1.035)
  other arithmetic: 25.7 us -> 34.6 us
  transfers between devices with their start and end apart: 19 -> 19, of which waited for: 7 -> 7; matrix products, arithmetic and copies ran while one was open for 5% -> 7% of each run, Pallas kernels for 59% -> 57%
where the time goes in v1:
time: 326 us; the launch traced here: 324 us
  Pallas kernels  229 us (70%)
  other arithmetic  34.6 us (11%)
  waiting for transfers between devices  25.1 us (8%)
  local copies, waits for them, and re-layouts  14 us (4%)
  starting transfers between devices  14 us (4%)
  between operations  5.14 us (2%)
    pallas_call x2, Pallas kernels, logits_pass(): pl.pallas_call(functools.partial(logits_body, shard, target), out_shape=(...  66.4 us
    pallas_call x2, Pallas kernels, embed_pass(): pl.pallas_call(functools.partial(embed_body, start), out_shape=(jax.Shape...  55.4 us
    pallas_call x1, Pallas kernels, hidden_pass(): pl.pallas_call(functools.partial(hidden_body, shard), out_shape=(jax.Shap...  40 us
    pallas_call x1, Pallas kernels, scatter_pass(): pl.pallas_call(functools.partial(scatter_body, per), out_shape=jax.ShapeD...  15.9 us
    pallas_call x1, Pallas kernels, gather_pass(): pl.pallas_call(functools.partial(gather_body, per), out_shape=jax.ShapeDt...  15.7 us
    pallas_call x1, Pallas kernels, back_pass(): pl.pallas_call(back_body, out_shape=(jax.ShapeDtypeStruct(old.shape, F32)...  15.2 us
    ppermute x5, waiting for transfers between devices, swap_dp(): return lax.ppermute(x, 'dp', SWAP_DP)  14.6 us
    pallas_call x1, Pallas kernels, transform_pass(): pl.pallas_call(transform_body, out_shape=(jax.ShapeDtypeStruct((MAIN, wid...  14.2 us
  transfers between devices with their start and end apart: 19, of which 7 were waited for; matrix products, arithmetic and copies ran while one was open for 7% of the time, Pallas kernels for 57%

profile of v1, /device:TPU:0, one launch (start us, length us, event | category | flops | bytes accessed | tf_op | source)
XLA Modules:
  0.0 324.1 jit_solution(16358020429695406869)
XLA Ops:
  0.6 0.8 reduce_sum.111
  2.1 1.9 add_bitcast_fusion
  4.6 3.4 %collective-permute-start.15 = (s32[8,128]{1,0:T(8,128)S(1)}, s32[8,128]{1,0:T(8,128)S(1)}, u32[]{:S(2)}, u32[]{:S(2)}) collective-permute-start(s32[8,128]{1,0:T(8,128)S(1)} %broadcast_in_dim.211), channel_id=1, source_target_pairs={{0,4},{4,0},{1,5},{5,1},{2,6},{6,2},{3,7},{7,3}} | collective-permute-start | bytes 12296 | tf_op jit(solution)/shard_map/ppermute | solution.py:36
  8.0 0.8 select_convert_fusion
  9.5 15.7 %shard_map.172 = bf16[3072,768]{1,0:T(8,128)(2,1)} custom-call(s32[32]{0:T(128)} %get-tuple-element.655.meta_ref, f32[32,1,128]{2,1,0:T(1,128)} %bitcast.100, bf16[32,512,768]{2,1,0:T(8,128)(2,1)} %h_ref.1), custom_call_target="tpu_custom_call" | custom-call | flops 3221225472 | bytes 25165824 | tf_op jit(solution)/shard_map/pallas_call | solution.py:71
  30.9 0.9 broadcast_in_dim.209
  32.4 266.9 %while.23 = (s32[]{:T(128)}, f32[7648,768]{1,0:T(8,128)}, f32[3328,768]{1,0:T(8,128)}, f32[200,768]{1,0:T(8,128)}, f32[1,7680]{1,0:T(1,128)}, /*index=5*/f32[]{:...) while((s32[]{:T(128)}, f32[7648,768]{1,0:T(8,128)}, ...), condition=%wide.wide.region_13.14_spmd.clone, body=%wide.wide.region_3.13_spmd.sunk.clone.sunk | while | flops 95857770496 | bytes 437659072 | solution.py:522
  32.4 0.8 select_reduce_fusion.7
  33.9 1.2 fusion.38
  35.7 14.2 %body.32 = (bf16[1536,768]{1,0:T(8,128)(2,1)}, bf16[768,1536]{1,0:T(8,128)(2,1)}, f32[1536,768]{1,0:T(8,128)}, f32[1536,768]{1,0:T(8,128)}, f32[384,768]{1,0:T(8,128)}) custom-call(s32[2]{0:T(128)} %pad_add_fusion.7.meta_ref, bf16[3072,768]{1,0:T(8,128)(2,1)} %get-tuple-element.1189.h_ref, bf16[768,768]{1,0:T(8,128)(2,1)} %get-tuple-element.1190.w_ref, ...), custom_call_target="tpu_custom_call" | custom-call | flops 1811939328 | bytes 16515072 | tf_op jit(solution)/shard_map/while/body/pallas_call | solution.py:119
  49.9 2.0 collective-permute-start
  52.5 34.5 %body.33 = (f32[7680,1536]{1,0:T(8,128)}, f32[120,1536]{1,0:T(8,128)}) custom-call(bf16[7648,768]{1,0:T(8,128)(2,1)} %get-tuple-element.1197.e_ref, bf16[768,1536]{1,0:T(8,128)(2,1)} %get-tuple-element.1053.t_ref, f32[1,7680]{1,0:T(1,128)S(1)} %get-tuple-element.1198.bias_ref, s32[1,1536]{1,0:T(1,128)} %and_select_fusion.8.lab_ref), custom_call_target="tpu_custom_call" | custom-call | flops 18043895808 | bytes 46989312 | tf_op jit(solution)/shard_map/while/body/pallas_call | solution.py:302
  87.0 2.2 slice_reduce_fusion.25
  90.1 1.9 fusion.39
  93.2 1.5 collective-permute-start.5
  95.9 1.5 collective-permute-done.5
  97.4 2.2 slice_reduce_fusion.27
  99.5 0.9 multiply_bitcast_fusion.6
  100.5 1.8 bitcast_select_fusion.6.vec_ref
  102.2 40.0 %body.34 = (bf16[7680,1536]{1,0:T(8,128)(2,1)}, f32[384,1536]{1,0:T(8,128)}, f32[384,1536]{1,0:T(8,128)}, f32[1,7680]{1,0:T(1,128)}) custom-call(s32[1]{0:T(128)} %bitcast.85.core_ref, f32[7680,1536]{1,0:T(8,128)} %get-tuple-element.1056.soft_ref, f32[120,1536]{1,0:T(8,128)} %bitcast_select_fusion.6.vec_ref, s32[1,1536]{1,0:T(1,128)} %and_select_fusion.8.lab_ref, ...), custom_call_target="tpu_custom_call" | custom-call | flops 18043895808 | bytes 70483968 | tf_op jit(solution)/shard_map/while/body/pallas_call | solution.py:356
  142.3 2.8 collective-permute-done.6.refs_3_
  145.2 1.2 broadcast_xor_fusion.3.place_ref
  147.7 6.2 %body.35 = (bf16[1536,768]{1,0:T(8,128)(2,1)}, bf16[768,1536]{1,0:T(8,128)(2,1)}) custom-call(s32[4]{0:T(128)} %broadcast_xor_fusion.3.place_ref, f32[384,768]{1,0:T(8,128)} %copy-done.8, f32[384,768]{1,0:T(8,128)} %copy-done.9, f32[384,768]{1,0:T(8,128)} %copy-done.10, f32[384,768]{1,0:T(8,128)} %copy-done.11), custom_call_target="tpu_custom_call" | custom-call | flops 1179648 | bytes 9437184 | tf_op jit(solution)/shard_map/while/body/pallas_call | solution.py:149
  153.9 2.3 slice_add_fusion.10
  156.5 1.6 collective-permute-start.8
  158.1 31.9 %body.36 = (f32[7680,1536]{1,0:T(8,128)}, f32[120,1536]{1,0:T(8,128)}) custom-call(bf16[7648,768]{1,0:T(8,128)(2,1)} %get-tuple-element.1197.e_ref, bf16[768,1536]{1,0:T(8,128)(2,1)} %get-tuple-element.1079.t_ref, f32[1,7680]{1,0:T(1,128)} %copy-done.33, s32[1,1536]{1,0:T(1,128)} %broadcast_in_dim.327.lab_ref), custom_call_target="tpu_custom_call" | custom-call | flops 18043895808 | bytes 46989312 | tf_op jit(solution)/shard_map/while/body/pallas_call | solution.py:302
  190.0 3.2 collective-permute-done.8
  193.3 2.4 slice_reduce_fusion.28
  195.8 1.2 collective-permute-done.9
  197.1 1.5 collective-permute-start.10
  198.5 1.8 add.457.mine_a_ref
  201.7 1.5 collective-permute-start.11
  203.2 1.0 bitcast_select_fusion.7.vec_ref
  204.2 26.3 %body.37 = (f32[7648,768]{1,0:T(8,128)}, f32[1,3584]{1,0:T(1,128)}) custom-call(s32[1]{0:T(128)} %bitcast.86.meta_ref, bf16[7680,1536]{1,0:T(8,128)(2,1)} %get-tuple-element.1096.dz_ref, f32[7680,1536]{1,0:T(8,128)} %get-tuple-element.1097.soft_ref, f32[120,1536]{1,0:T(8,128)} %bitcast_select_fusion.7.vec_ref, ...), custom_call_target="tpu_custom_call", output_to_operand_aliasing={{0}: (8, {})} | custom-call | flops 16911433728 | bytes 44040192 | tf_op jit(solution)/shard_map/while/body/pallas_call | solution.py:390
  230.6 1.1 copy-done.3
  231.8 1.3 add.458.mine_b_ref
  233.8 1.3 select_reduce_fusion.8
  235.8 0.9 copy-done.13
  236.6 15.2 %body.38 = (f32[3328,768]{1,0:T(8,128)}, f32[800,768]{1,0:T(8,128)}) custom-call(s32[2]{0:T(128)} %pad_add_fusion.6.meta_ref, f32[384,1024]{1,0:T(8,128)} %copy-done, f32[384,1024]{1,0:T(8,128)} %copy-done.3, f32[384,512]{1,0:T(8,128)} %copy-done.1, f32[384,512]{1,0:T(8,128)} %copy-done.13, ...), custom_call_target="tpu_custom_call", output_to_operand_aliasing={{0}: (10, {})} | custom-call | flops 3623878656 | bytes 21233664 | tf_op jit(solution)/shard_map/while/body/pallas_call | solution.py:203
  251.8 1.1 constant_dynamic-slice_fusion.3
  252.9 29.2 %body.39 = (f32[7648,768]{1,0:T(8,128)}, f32[1,4096]{1,0:T(1,128)}) custom-call(s32[1]{0:T(128)} %bitcast.86.meta_ref, bf16[7680,1536]{1,0:T(8,128)(2,1)} %get-tuple-element.1096.dz_ref, f32[7680,1536]{1,0:T(8,128)} %get-tuple-element.1097.soft_ref, f32[120,1536]{1,0:T(8,128)} %bitcast_select_fusion.7.vec_ref, ...), custom_call_target="tpu_custom_call", output_to_operand_aliasing={{0}: (8, {})} | custom-call | flops 19327352832 | bytes 50331648 | tf_op jit(solution)/shard_map/while/body/pallas_call | solution.py:390
  282.9 0.8 maximum_add_fusion.3
  283.6 14.6 %collective-permute-done.14 = f32[200,768]{1,0:T(8,128)S(1)} collective-permute-done((f32[200,768]{1,0:T(8,128)S(1)}, f32[200,768]{1,0:T(8,128)S(1)}, u32[]{:S(2)}, u32[]{:S(2)}) %collective-permute-start.14) | collective-permute-done | bytes 614432 | tf_op jit(solution)/shard_map/while/body/ppermute | solution.py:36
  298.5 0.8 copy-done.5
  300.4 15.9 %shard_map.173 = bf16[32,512,768]{2,1,0:T(8,128)(2,1)} custom-call(s32[32]{0:T(128)} %get-tuple-element.654.meta_ref, f32[32,1,128]{2,1,0:T(1,128)} %bitcast.101, f32[3328,768]{1,0:T(8,128)} %get-tuple-element.398.dh_ref), custom_call_target="tpu_custom_call" | custom-call | flops 3221225472 | bytes 25165824 | tf_op jit(solution)/shard_map/pallas_call | solution.py:236
  316.3 1.1 maximum_select_fusion.2
  319.5 1.1 collective-permute-done.18
  320.8 1.6 slice.246
  (158 shorter events, 19.0 us)
Async XLA Ops:
  4.6 23.2 %collective-permute-start.15 = (s32[8,128]{1,0:T(8,128)S(1)}, s32[8,128]{1,0:T(8,128)S(1)}, u32[]{:S(2)}, u32[]{:S(2)}) collective-permute-start(s32[8,128]{1,0:T(8,128)S(1)} %broadcast_in_dim.211), channel_id=1, source_target_pairs={{0,4},{4,0},{1,5},{5,1},{2,6},{6,2},{3,7},{7,3}} | collective-permute-start | bytes 12296 | tf_op jit(solution)/shard_map/ppermute | solution.py:36
  32.4 20.1 %copy-start.33 = (f32[1,7680]{1,0:T(1,128)}, f32[1,7680]{1,0:T(1,128)S(1)}, u32[]{:S(2)}) copy-start(f32[1,7680]{1,0:T(1,128)S(1)} %get-tuple-element.1198.bias_ref) | copy-start | bytes 92164 | tf_op jit(solution)/shard_map/while
  35.1 51.9 %collective-permute-start.1 = (s32[1536]{0:T(1024)S(1)}, s32[1536]{0:T(1024)S(1)}, u32[]{:S(2)}, u32[]{:S(2)}) collective-permute-start(s32[1536]{0:T(1024)S(1)} %convert_element_type.63), channel_id=1, source_target_pairs={{0,4},{4,0},{1,5},{5,1},{2,6},{6,2},{3,7},{7,3}} | collective-permute-start | bytes 18440 | tf_op jit(solution)/shard_map/while/body/ppermute | solution.py:36
  49.9 37.1 %collective-permute-start = (f32[384,768]{1,0:T(8,128)}, f32[384,768]{1,0:T(8,128)S(1)}, u32[]{:S(2)}, u32[]{:S(2)}) collective-permute-start(f32[384,768]{1,0:T(8,128)} %get-tuple-element.1052), channel_id=1, source_target_pairs={{0,4},{4,0},{1,5},{5,1},{2,6},{6,2},{3,7},{7,3}} | collective-permute-start | bytes 3538952 | tf_op jit(solution)/shard_map/while/body/ppermute | solution.py:36
  87.0 7.7 %copy-start.29 = (s32[1536]{0:T(1024)}, s32[1536]{0:T(1024)S(1)}, u32[]{:S(2)}) copy-start(s32[1536]{0:T(1024)S(1)} %collective-permute-done.1) | copy-start | bytes 18436 | tf_op jit(solution)/shard_map/while
  87.0 55.1 %copy-start.8 = (f32[384,768]{1,0:T(8,128)}, f32[384,768]{1,0:T(8,128)S(1)}, u32[]{:S(2)}) copy-start(f32[384,768]{1,0:T(8,128)S(1)} %collective-permute-done.refs_0_) | copy-start | bytes 3538948 | tf_op jit(solution)/shard_map/while
  89.3 5.4 %copy-start.14 = (f32[1536]{0:T(1024)}, f32[1536]{0:T(1024)S(1)}, u32[]{:S(2)}) copy-start(f32[1536]{0:T(1024)S(1)} %get-tuple-element.1060) | copy-start | bytes 18436 | tf_op jit(solution)/shard_map/while
  90.0 1.9 collective-permute-start.4
  92.6 2.1 copy-start.19
  92.6 2.1 copy-start.20
  93.2 4.1 %collective-permute-start.5 = (f32[3,1536]{1,0:T(4,128)}, f32[3,1536]{1,0:T(4,128)}, u32[]{:S(2)}, u32[]{:S(2)}) collective-permute-start(f32[3,1536]{1,0:T(4,128)} %pad_maximum_fusion.16), channel_id=1, source_target_pairs={{0,2},{1,3},{2,0},{3,1},{4,6},{5,7},{6,4},{7,5}} | collective-permute-start | bytes 55304 | tf_op jit(solution)/shard_map/while/body/ppermute | solution.py:44
  95.3 46.8 %collective-permute-start.2 = (f32[384,768]{1,0:T(8,128)S(1)}, f32[384,768]{1,0:T(8,128)S(1)}, u32[]{:S(2)}, u32[]{:S(2)}) collective-permute-start(f32[384,768]{1,0:T(8,128)S(1)} %collective-permute-done.refs_0_), channel_id=1, source_target_pairs={{0,2},{1,3},{2,0},{3,1},{4,6},{5,7},{6,4},{7,5}} | collective-permute-start | bytes 3538952 | tf_op jit(solution)/shard_map/while/body/ppermute | solution.py:44
  95.9 46.3 %collective-permute-start.3 = (f32[384,768]{1,0:T(8,128)S(1)}, f32[384,768]{1,0:T(8,128)S(1)}, u32[]{:S(2)}, u32[]{:S(2)}) collective-permute-start(f32[384,768]{1,0:T(8,128)S(1)} %collective-permute-done.refs_0_), channel_id=1, source_target_pairs={{0,1},{1,0},{2,3},{3,2},{4,5},{5,4},{6,7},{7,6}} | collective-permute-start | bytes 3538952 | tf_op jit(solution)/shard_map/while/body/ppermute | solution.py:40
  142.2 2.9 copy-start.9
  142.2 2.9 copy-start.10
  142.2 2.9 collective-permute-start.6
  145.1 2.6 copy-start.11
  145.1 8.8 %collective-permute-start.7 = (f32[384,1536]{1,0:T(8,128)}, f32[384,1536]{1,0:T(8,128)S(1)}, u32[]{:S(2)}, u32[]{:S(2)}) collective-permute-start(f32[384,1536]{1,0:T(8,128)} %get-tuple-element.1071), channel_id=1, source_target_pairs={{0,1},{1,0},{2,3},{3,2},{4,5},{5,4},{6,7},{7,6}} | collective-permute-start | bytes 7077896 | tf_op jit(solution)/shard_map/while/body/ppermute | solution.py:40
  153.9 2.4 copy-start.2
  156.5 36.8 %collective-permute-start.8 = (f32[384,1024]{1,0:T(8,128)S(1)}, f32[384,1024]{1,0:T(8,128)S(1)}, u32[]{:S(2)}, u32[]{:S(2)}) collective-permute-start(f32[384,1024]{1,0:T(8,128)S(1)} %slice_add_fusion.9), channel_id=1, source_target_pairs={{0,2},{1,3},{2,0},{3,1},{4,6},{5,7},{6,4},{7,5}} | collective-permute-start | bytes 4718600 | tf_op jit(solution)/shard_map/while/body/ppermute | solution.py:44
  193.3 3.8 %copy-start.7 = (f32[384,1024]{1,0:T(8,128)}, f32[384,1024]{1,0:T(8,128)S(1)}, u32[]{:S(2)}) copy-start(f32[384,1024]{1,0:T(8,128)S(1)} %collective-permute-done.8) | copy-start | bytes 4718596 | tf_op jit(solution)/shard_map/while
  195.8 1.2 collective-permute-start.9
  197.1 6.1 %copy-start.21 = (f32[1536]{0:T(1024)S(1)}, f32[1536]{0:T(1024)}, u32[]{:S(2)}) copy-start(f32[1536]{0:T(1024)} %get-tuple-element.1098) | copy-start | bytes 18436 | tf_op jit(solution)/shard_map/while
  197.1 6.1 %copy-start.30 = (pred[120]{0:T(512)(128)(4,1)S(1)}, pred[120]{0:T(512)(128)(4,1)}, u32[]{:S(2)}) copy-start(pred[120]{0:T(512)(128)(4,1)} %broadcast_in_dim.326) | copy-start | bytes 364 | tf_op jit(solution)/shard_map/while
  197.1 3.8 %collective-permute-start.10 = (f32[3,1536]{1,0:T(4,128)S(1)}, f32[3,1536]{1,0:T(4,128)S(1)}, u32[]{:S(2)}, u32[]{:S(2)}) collective-permute-start(f32[3,1536]{1,0:T(4,128)S(1)} %pad_maximum_fusion.18), channel_id=1, source_target_pairs={{0,2},{1,3},{2,0},{3,1},{4,6},{5,7},{6,4},{7,5}} | collective-permute-start | bytes 55304 | tf_op jit(solution)/shard_map/while/body/ppermute | solution.py:44
  200.3 30.2 %copy-start = (f32[384,1024]{1,0:T(8,128)}, f32[384,1024]{1,0:T(8,128)S(1)}, u32[]{:S(2)}) copy-start(f32[384,1024]{1,0:T(8,128)S(1)} %add.457.mine_a_ref) | copy-start | bytes 4718596 | tf_op jit(solution)/shard_map/while
  200.3 30.3 %collective-permute-start.12 = (f32[384,1024]{1,0:T(8,128)S(1)}, f32[384,1024]{1,0:T(8,128)S(1)}, u32[]{:S(2)}, u32[]{:S(2)}) collective-permute-start(f32[384,1024]{1,0:T(8,128)S(1)} %add.457.mine_a_ref), channel_id=1, source_target_pairs={{0,1},{1,0},{2,3},{3,2},{4,5},{5,4},{6,7},{7,6}} | collective-permute-start | bytes 4718600 | tf_op jit(solution)/shard_map/while/body/ppermute | solution.py:40
  201.7 28.9 %collective-permute-start.11 = (f32[384,512]{1,0:T(8,128)}, f32[384,512]{1,0:T(8,128)S(1)}, u32[]{:S(2)}, u32[]{:S(2)}) collective-permute-start(f32[384,512]{1,0:T(8,128)} %slice_add_fusion.10), channel_id=1, source_target_pairs={{0,2},{1,3},{2,0},{3,1},{4,6},{5,7},{6,4},{7,5}} | collective-permute-start | bytes 2359304 | tf_op jit(solution)/shard_map/while/body/ppermute | solution.py:44
  230.5 3.3 %copy-start.15 = (f32[1536]{0:T(1024)S(1)}, f32[1536]{0:T(1024)}, u32[]{:S(2)}) copy-start(f32[1536]{0:T(1024)} %copy-done.14) | copy-start | bytes 18436 | tf_op jit(solution)/shard_map/while
  230.5 3.3 %copy-start.22 = (f32[1536]{0:T(1024)S(1)}, f32[1536]{0:T(1024)}, u32[]{:S(2)}) copy-start(f32[1536]{0:T(1024)} %get-tuple-element.1123) | copy-start | bytes 18436 | tf_op jit(solution)/shard_map/while
  230.5 3.3 %copy-start.23 = (f32[1536]{0:T(1024)S(1)}, f32[1536]{0:T(1024)}, u32[]{:S(2)}) copy-start(f32[1536]{0:T(1024)} %get-tuple-element.1122) | copy-start | bytes 18436 | tf_op jit(solution)/shard_map/while
  230.5 3.3 %copy-start.24 = (f32[1536]{0:T(1024)S(1)}, f32[1536]{0:T(1024)}, u32[]{:S(2)}) copy-start(f32[1536]{0:T(1024)} %get-tuple-element.1120) | copy-start | bytes 18436 | tf_op jit(solution)/shard_map/while
  230.5 3.3 %copy-start.25 = (f32[1536]{0:T(1024)S(1)}, f32[1536]{0:T(1024)}, u32[]{:S(2)}) copy-start(f32[1536]{0:T(1024)} %get-tuple-element.1125) | copy-start | bytes 18436 | tf_op jit(solution)/shard_map/while
  230.6 3.3 %copy-start.26 = (f32[1536]{0:T(1024)S(1)}, f32[1536]{0:T(1024)}, u32[]{:S(2)}) copy-start(f32[1536]{0:T(1024)} %get-tuple-element.1124) | copy-start | bytes 18436 | tf_op jit(solution)/shard_map/while
  230.6 3.3 %copy-start.27 = (f32[1536]{0:T(1024)S(1)}, f32[1536]{0:T(1024)}, u32[]{:S(2)}) copy-start(f32[1536]{0:T(1024)} %get-tuple-element.1121) | copy-start | bytes 18436 | tf_op jit(solution)/shard_map/while
  230.6 6.1 %copy-start.31 = (f32[1,768]{1,0:T(1,128)S(1)}, f32[1,768]{1,0:T(1,128)}, u32[]{:S(2)}) copy-start(f32[1,768]{1,0:T(1,128)} %get-tuple-element.1203.gamma_ref) | copy-start | bytes 9220 | tf_op jit(solution)/shard_map/while
  233.0 2.7 copy-start.1
  233.0 2.7 collective-permute-start.13
  252.9 30.0 %copy-start.16 = (f32[1,7680]{1,0:T(1,128)S(1)}, f32[1,7680]{1,0:T(1,128)}, u32[]{:S(2)}) copy-start(f32[1,7680]{1,0:T(1,128)} %get-tuple-element.1157) | copy-start | bytes 92164 | tf_op jit(solution)/shard_map/while
  252.9 29.9 %copy-start.28 = (f32[1,3584]{1,0:T(1,128)S(1)}, f32[1,3584]{1,0:T(1,128)}, u32[]{:S(2)}) copy-start(f32[1,3584]{1,0:T(1,128)} %get-tuple-element.1119) | copy-start | bytes 43012 | tf_op jit(solution)/shard_map/while
  252.9 45.4 %copy-start.4 = (f32[200,768]{1,0:T(8,128)S(1)}, f32[200,768]{1,0:T(8,128)}, u32[]{:S(2)}) copy-start(f32[200,768]{1,0:T(8,128)} %get-tuple-element.1156) | copy-start | bytes 1843204 | tf_op jit(solution)/shard_map/while
  282.1 17.3 %copy-start.34 = (f32[1,7680]{1,0:T(1,128)S(1)}, f32[1,7680]{1,0:T(1,128)}, u32[]{:S(2)}) copy-start(f32[1,7680]{1,0:T(1,128)} %copy-done.33) | copy-start | bytes 92164 | tf_op jit(solution)/shard_map/while
  282.1 16.2 %collective-permute-start.14 = (f32[200,768]{1,0:T(8,128)S(1)}, f32[200,768]{1,0:T(8,128)S(1)}, u32[]{:S(2)}, u32[]{:S(2)}) collective-permute-start(f32[200,768]{1,0:T(8,128)S(1)} %constant_dynamic-slice_fusion.3), channel_id=1, source_target_pairs={{0,4},{4,0},{1,5},{5,1},{2,6},{6,2},{3,7},{7,3}} | collective-permute-start | bytes 1843208 | tf_op jit(solution)/shard_map/while/body/ppermute | solution.py:36
  283.6 14.9 %copy-start.17 = (f32[1,7680]{1,0:T(1,128)}, f32[1,7680]{1,0:T(1,128)S(1)}, u32[]{:S(2)}) copy-start(f32[1,7680]{1,0:T(1,128)S(1)} %maximum_add_fusion.3) | copy-start | bytes 92164 | tf_op jit(solution)/shard_map/while
  299.4 17.0 %collective-permute-start.16 = (f32[200,768]{1,0:T(8,128)}, f32[200,768]{1,0:T(8,128)S(1)}, u32[]{:S(2)}, u32[]{:S(2)}) collective-permute-start(f32[200,768]{1,0:T(8,128)} %get-tuple-element.397), channel_id=1, source_target_pairs={{0,2},{1,3},{2,0},{3,1},{4,6},{5,7},{6,4},{7,5}} | collective-permute-start | bytes 1843208 | tf_op jit(solution)/shard_map/ppermute | solution.py:44
  300.0 16.4 %collective-permute-start.17 = (f32[8,128]{1,0:T(8,128)S(1)}, f32[8,128]{1,0:T(8,128)S(1)}, u32[]{:S(2)}, u32[]{:S(2)}) collective-permute-start(f32[8,128]{1,0:T(8,128)S(1)} %broadcast_in_dim.226), channel_id=1, source_target_pairs={{0,4},{4,0},{1,5},{5,1},{2,6},{6,2},{3,7},{7,3}} | collective-permute-start | bytes 12296 | tf_op jit(solution)/shard_map/ppermute | solution.py:36
  300.4 15.9 %copy-start.6 = (f32[200,768]{1,0:T(8,128)S(1)}, f32[200,768]{1,0:T(8,128)}, u32[]{:S(2)}) copy-start(f32[200,768]{1,0:T(8,128)} %get-tuple-element.397) | copy-start | bytes 1843204
  317.5 3.1 collective-permute-start.18
  (10 other events, 10.5 us)

commit v2 on v1

--- a/solution.py
+++ b/solution.py
@@ -20,7 +20,7 @@
 SUB = 64
 BACK = 256
 WIN = 128
-VMEM_LIMIT = 60 * 1024 * 1024
+VMEM_LIMIT = 44 * 1024 * 1024
 
 SWAP_DP = tuple((i, i ^ 1) for i in range(2))
 SWAP_CORE = tuple((i, i ^ 1) for i in range(4))
@@ -371,16 +371,28 @@
     )(core.reshape(1), soft, vec, lab, embed)
 
 
-def embed_body(start, meta_ref, dz_ref, soft_ref, vec_ref, lab_ref, t_own_ref, t_oth_ref, db_own_ref, old_ref, de_ref, db_ref, dz_s):
+def embed_body(start, meta_ref, dz_ref, soft_ref, vec_ref, lab_ref, t_own_ref, t_oth_ref, db_own_ref, old_ref, de_ref, db_ref, dz_s, old_s, sem):
     step = pl.program_id(0) + start
+    tail = old_ref.shape[0] % VT
+
+    @pl.when(pl.program_id(0) == 0)
+    def _():
+        old_s[...] = jnp.zeros_like(old_s)
+
+    for rows, here in ((VT, step < old_ref.shape[0] // VT), (tail, step == old_ref.shape[0] // VT)):
+        @pl.when((meta_ref[0] > 0) & here)
+        def _():
+            copy = pltpu.make_async_copy(old_ref.at[pl.ds(pl.multiple_of(step * VT, VT), rows)], old_s.at[:rows], sem)
+            copy.start()
+            copy.wait()
+
     vocab = lax.broadcasted_iota(jnp.int32, (VT, CB), 0)
     acc = []
     for cols in columns():
         dz = grad_logits(soft_ref, vec_ref, lab_ref, cols, vocab, step)
         acc.append(lane_groups(dz))
         dz_s[:, cols] = dz.astype(BF16)
-    old = jnp.where(meta_ref[0] == 0, 0.0, old_ref[...])
-    de_ref[...] = old + jnp.dot(dz_ref[...], t_own_ref[...], preferred_element_type=F32)
+    de_ref[...] = old_s[...] + jnp.dot(dz_ref[...], t_own_ref[...], preferred_element_type=F32)
     de_ref[...] += jnp.dot(dz_s[...], t_oth_ref[...], preferred_element_type=F32)
     db_ref[...] = db_own_ref[...] + jnp.sum(sum(acc[1:], acc[0]).T, axis=0, keepdims=True)
 
@@ -394,10 +406,10 @@
             num_scalar_prefetch=1, grid=(count,),
             in_specs=[
                 by_tile(VT, MAIN, start), by_tile(VT, MAIN, start), by_tile(8, MAIN, start), whole(1, MAIN),
-                whole(MAIN, width), whole(MAIN, width), strip_of(start), by_tile(VT, width, start),
+                whole(MAIN, width), whole(MAIN, width), strip_of(start), pl.BlockSpec(memory_space=pl.ANY),
             ],
             out_specs=(by_tile(VT, width, start), strip_of()),
-            scratch_shapes=[pltpu.VMEM((VT, MAIN), BF16)],
+            scratch_shapes=[pltpu.VMEM((VT, MAIN), BF16), pltpu.VMEM((VT, width), F32), pltpu.SemaphoreType.DMA],
         ),
         input_output_aliases={8: 0},
         compiler_params=params(),

time: 326 us -> 298 us (0.914)
  other arithmetic: 34.6 us -> 16.9 us
  Pallas kernels: 229 us -> 212 us
  waiting for transfers between devices: 25.1 us -> 30.6 us
    pallas_call x2, Pallas kernels: 55.4 us -> 49.2 us  [embed_pass(): pl.pallas_call(functools.partial(embed_body, start), out_shape=(jax.Shape...]
    pallas_call x1, Pallas kernels: 6.18 us -> 1.81 us  [collect_pass(): pl.pallas_call(collect_body, out_shape=(jax.ShapeDtypeStruct((MAIN, width...]
    while x64 -> x86, local copies, waits for them, and re-layouts: 3.59 us -> 6.67 us
  transfers between devices with their start and end apart: 19 -> 19, of which waited for: 7 -> 9; matrix products, arithmetic and copies ran while one was open for 7% -> 4% of each run, Pallas kernels for 57% -> 58%
where the time goes in v2:
time: 298 us; the launch traced here: 297 us
  Pallas kernels  212 us (71%)
  waiting for transfers between devices  30.6 us (10%)
  other arithmetic  16.9 us (6%)
  local copies, waits for them, and re-layouts  16.1 us (5%)
  starting transfers between devices  14.2 us (5%)
  between operations  5.19 us (2%)
    pallas_call x2, Pallas kernels, logits_pass(): pl.pallas_call(functools.partial(logits_body, shard, target), out_shape=(...  65.3 us
    pallas_call x2, Pallas kernels, embed_pass(): pl.pallas_call(functools.partial(embed_body, start), out_shape=(jax.Shape...  49.2 us
    pallas_call x1, Pallas kernels, hidden_pass(): pl.pallas_call(functools.partial(hidden_body, shard), out_shape=(jax.Shap...  37.8 us
    pallas_call x1, Pallas kernels, scatter_pass(): pl.pallas_call(functools.partial(scatter_body, per), out_shape=jax.ShapeD...  15.6 us
    pallas_call x1, Pallas kernels, gather_pass(): pl.pallas_call(functools.partial(gather_body, per), out_shape=jax.ShapeDt...  15.5 us
    ppermute x5, waiting for transfers between devices, swap_dp(): return lax.ppermute(x, 'dp', SWAP_DP)  15.2 us
    pallas_call x1, Pallas kernels, back_pass(): pl.pallas_call(back_body, out_shape=(jax.ShapeDtypeStruct(old.shape, F32)...  13.5 us
    pallas_call x1, Pallas kernels, transform_pass(): pl.pallas_call(transform_body, out_shape=(jax.ShapeDtypeStruct((MAIN, wid...  13.4 us
  transfers between devices with their start and end apart: 19, of which 9 were waited for; matrix products, arithmetic and copies ran while one was open for 4% of the time, Pallas kernels for 58%

profile of v2, /device:TPU:0, one launch (start us, length us, event | category | flops | bytes accessed | tf_op | source)
XLA Modules:
  0.0 296.9 jit_solution(15424937770510706527)
XLA Ops:
  0.6 0.8 reduce_sum.111
  2.2 0.6 broadcast_in_dim.211
  2.9 3.4 %collective-permute-start.15 = (s32[8,128]{1,0:T(8,128)S(1)}, s32[8,128]{1,0:T(8,128)S(1)}, u32[]{:S(2)}, u32[]{:S(2)}) collective-permute-start(s32[8,128]{1,0:T(8,128)S(1)} %broadcast_in_dim.211), channel_id=1, source_target_pairs={{0,4},{4,0},{1,5},{5,1},{2,6},{6,2},{3,7},{7,3}} | collective-permute-start | bytes 12296 | tf_op jit(solution)/shard_map/ppermute | solution.py:36
  6.3 0.8 select_convert_fusion
  7.2 15.5 %shard_map.172 = bf16[3072,768]{1,0:T(8,128)(2,1)} custom-call(s32[32]{0:T(128)S(1)} %get-tuple-element.655.meta_ref, f32[32,1,128]{2,1,0:T(1,128)S(1)} %bitcast.93, bf16[32,512,768]{2,1,0:T(8,128)(2,1)} %h_ref.1), custom_call_target="tpu_custom_call" | custom-call | flops 3221225472 | bytes 25165824 | tf_op jit(solution)/shard_map/pallas_call | solution.py:71
  27.8 0.9 broadcast_in_dim.209
  29.3 242.5 %while.23 = (s32[]{:T(128)}, f32[7648,768]{1,0:T(8,128)}, f32[3328,768]{1,0:T(8,128)}, f32[200,768]{1,0:T(8,128)}, f32[1,7680]{1,0:T(1,128)}, /*index=5*/f32[]{:...) while((s32[]{:T(128)}, f32[7648,768]{1,0:T(8,128)}, ...), condition=%wide.wide.region_13.14_spmd.clone, body=%wide.wide.region_3.13_spmd.sunk.clone.sunk | while | flops 95857770496 | bytes 428814144 | solution.py:534
  29.4 0.7 subtract_select_fusion.3
  30.7 13.4 %body.32 = (bf16[1536,768]{1,0:T(8,128)(2,1)S(1)}, bf16[768,1536]{1,0:T(8,128)(2,1)S(1)}, f32[1536,768]{1,0:T(8,128)}, f32[1536,768]{1,0:T(8,128)}, f32[384,768]{1,0:T(8,128)S(1)}) custom-call(s32[2]{0:T(128)S(1)} %pad_add_fusion.7.meta_ref, bf16[3072,768]{1,0:T(8,128)(2,1)} %get-tuple-element.1189.h_ref, bf16[768,768]{1,0:T(8,128)(2,1)} %get-tuple-element.1190.w_ref, ...), custom_call_target="tpu_custom_call" | custom-call | flops 1811939328 | bytes 16515072 | tf_op jit(solution)/shard_map/while/body/pallas_call | solution.py:119
  44.1 2.0 collective-permute-start
  46.1 34.3 %body.33 = (f32[7680,1536]{1,0:T(8,128)}, f32[120,1536]{1,0:T(8,128)S(1)}) custom-call(bf16[7648,768]{1,0:T(8,128)(2,1)} %get-tuple-element.1197.e_ref, bf16[768,1536]{1,0:T(8,128)(2,1)S(1)} %get-tuple-element.1053.t_ref, f32[1,7680]{1,0:T(1,128)S(1)} %copy-done.37, s32[1,1536]{1,0:T(1,128)S(1)} %and_select_fusion.8.lab_ref), custom_call_target="tpu_custom_call" | custom-call | flops 18043895808 | bytes 46989312 | tf_op jit(solution)/shard_map/while/body/pallas_call | solution.py:302
  82.1 1.9 fusion.39
  83.9 0.7 slice_reduce_fusion.26
  85.8 1.5 collective-permute-start.5
  88.5 1.5 collective-permute-done.5
  90.0 2.2 slice_reduce_fusion.27
  92.2 0.9 multiply_bitcast_fusion.6
  93.1 0.8 bitcast_select_fusion.6.vec_ref
  93.9 37.8 %body.34 = (bf16[7680,1536]{1,0:T(8,128)(2,1)}, f32[384,1536]{1,0:T(8,128)S(1)}, f32[384,1536]{1,0:T(8,128)S(1)}, f32[1,7680]{1,0:T(1,128)S(1)}) custom-call(s32[1]{0:T(128)} %bitcast.85.core_ref, f32[7680,1536]{1,0:T(8,128)} %get-tuple-element.1056.soft_ref, f32[120,1536]{1,0:T(8,128)S(1)} %bitcast_select_fusion.6.vec_ref, ...), custom_call_target="tpu_custom_call" | custom-call | flops 18043895808 | bytes 70483968 | tf_op jit(solution)/shard_map/while/body/pallas_call | solution.py:356
  131.8 2.8 collective-permute-done.6.refs_3_
  134.8 1.8 body.35
  136.6 2.5 collective-permute-done.7
  139.6 1.6 collective-permute-start.8
  141.2 31.0 %body.36 = (f32[7680,1536]{1,0:T(8,128)}, f32[120,1536]{1,0:T(8,128)S(1)}) custom-call(bf16[7648,768]{1,0:T(8,128)(2,1)} %get-tuple-element.1197.e_ref, bf16[768,1536]{1,0:T(8,128)(2,1)S(1)} %get-tuple-element.1079.t_ref, f32[1,7680]{1,0:T(1,128)S(1)} %copy-done.38, s32[1,1536]{1,0:T(1,128)S(1)} %broadcast_in_dim.327.lab_ref), custom_call_target="tpu_custom_call" | custom-call | flops 18043895808 | bytes 46989312 | tf_op jit(solution)/shard_map/while/body/pallas_call | solution.py:302
  172.3 3.8 %collective-permute-done.8 = f32[384,1024]{1,0:T(8,128)S(1)} collective-permute-done((f32[384,1024]{1,0:T(8,128)S(1)}, f32[384,1024]{1,0:T(8,128)S(1)}, u32[]{:S(2)}, u32[]{:S(2)}) %collective-permute-start.8) | collective-permute-done | bytes 1572896 | tf_op jit(solution)/shard_map/while/body/ppermute | solution.py:44
  176.4 1.2 collective-permute-done.9
  177.7 1.6 collective-permute-start.10
  179.7 1.8 collective-permute-done.10
  181.6 0.7 slice_reduce_fusion.29
  182.3 1.6 collective-permute-start.11
  184.1 23.2 %body.37 = (f32[7648,768]{1,0:T(8,128)}, f32[1,3584]{1,0:T(1,128)S(1)}) custom-call(s32[1]{0:T(128)} %bitcast.86.meta_ref, bf16[7680,1536]{1,0:T(8,128)(2,1)} %get-tuple-element.1096.dz_ref, f32[7680,1536]{1,0:T(8,128)} %get-tuple-element.1097.soft_ref, f32[120,1536]{1,0:T(8,128)S(1)} %bitcast_select_fusion.7.vec_ref, ...), custom_call_target="tpu_custom_call", output_to_operand_aliasing={{0}: (8, {})} | custom-call | flops 16911433728 | bytes 44040192 | tf_op jit(solution)/shard_map/while/body/pallas_call | solution.py:402
  207.5 1.1 copy-done.4
  208.6 1.1 add.458.mine_b_ref
  209.8 1.3 select_reduce_fusion.8
  211.6 0.7 collective-permute-done.13.theirs_b_ref
  212.3 1.4 copy-done.3
  213.7 1.4 copy-done.5
  215.1 13.5 %body.38 = (f32[3328,768]{1,0:T(8,128)}, f32[800,768]{1,0:T(8,128)S(1)}) custom-call(s32[2]{0:T(128)S(1)} %pad_add_fusion.6.meta_ref, f32[384,1024]{1,0:T(8,128)S(1)} %copy-done.3, f32[384,1024]{1,0:T(8,128)S(1)} %copy-done.5, f32[384,512]{1,0:T(8,128)} %add.458.mine_b_ref, ...), custom_call_target="tpu_custom_call", output_to_operand_aliasing={{0}: (10, {})} | custom-call | flops 3623878656 | bytes 21233664 | tf_op jit(solution)/shard_map/while/body/pallas_call | solution.py:203
  228.7 26.0 %body.39 = (f32[7648,768]{1,0:T(8,128)}, f32[1,4096]{1,0:T(1,128)S(1)}) custom-call(s32[1]{0:T(128)} %bitcast.86.meta_ref, bf16[7680,1536]{1,0:T(8,128)(2,1)} %get-tuple-element.1096.dz_ref, f32[7680,1536]{1,0:T(8,128)} %get-tuple-element.1097.soft_ref, f32[120,1536]{1,0:T(8,128)S(1)} %bitcast_select_fusion.7.vec_ref, ...), custom_call_target="tpu_custom_call", output_to_operand_aliasing={{0}: (8, {})} | custom-call | flops 19327352832 | bytes 50331648 | tf_op jit(solution)/shard_map/while/body/pallas_call | solution.py:402
  254.8 0.7 collective-permute-start.14
  255.5 15.2 %collective-permute-done.14 = f32[200,768]{1,0:T(8,128)S(1)} collective-permute-done((f32[200,768]{1,0:T(8,128)S(1)}, f32[200,768]{1,0:T(8,128)S(1)}, u32[]{:S(2)}, u32[]{:S(2)}) %collective-permute-start.14) | collective-permute-done | bytes 614432 | tf_op jit(solution)/shard_map/while/body/ppermute | solution.py:36
  271.0 0.8 copy-done.11
  272.7 0.7 copy-done.9
  273.4 15.6 %shard_map.173 = bf16[32,512,768]{2,1,0:T(8,128)(2,1)} custom-call(s32[32]{0:T(128)S(1)} %get-tuple-element.654.meta_ref, f32[32,1,128]{2,1,0:T(1,128)S(1)} %bitcast.94, f32[3328,768]{1,0:T(8,128)} %get-tuple-element.398.dh_ref), custom_call_target="tpu_custom_call" | custom-call | flops 3221225472 | bytes 25165824 | tf_op jit(solution)/shard_map/pallas_call | solution.py:236
  289.1 1.1 maximum_select_fusion.2
  290.2 0.7 slice_reduce_fusion.11
  292.2 1.1 collective-permute-done.18
  293.6 1.6 slice.246
  (184 shorter events, 13.1 us)
Async XLA Ops:
  2.9 21.8 %collective-permute-start.15 = (s32[8,128]{1,0:T(8,128)S(1)}, s32[8,128]{1,0:T(8,128)S(1)}, u32[]{:S(2)}, u32[]{:S(2)}) collective-permute-start(s32[8,128]{1,0:T(8,128)S(1)} %broadcast_in_dim.211), channel_id=1, source_target_pairs={{0,4},{4,0},{1,5},{5,1},{2,6},{6,2},{3,7},{7,3}} | collective-permute-start | bytes 12296 | tf_op jit(solution)/shard_map/ppermute | solution.py:36
  7.2 15.5 %copy-start.8 = (f32[32,128]{1,0:T(8,128)}, f32[32,128]{1,0:T(8,128)S(1)}, u32[]{:S(2)}) copy-start(f32[32,128]{1,0:T(8,128)S(1)} %select_select_fusion) | copy-start | bytes 49156
  29.3 14.8 %copy-start.39 = (f32[8,768]{1,0:T(8,128)}, f32[8,768]{1,0:T(8,128)S(1)}, u32[]{:S(2)}) copy-start(f32[8,768]{1,0:T(8,128)S(1)} %get-tuple-element.1191.vec_ref) | copy-start | bytes 73732 | tf_op jit(solution)/shard_map/while
  30.6 49.9 %collective-permute-start.1 = (s32[1536]{0:T(1024)S(1)}, s32[1536]{0:T(1024)S(1)}, u32[]{:S(2)}, u32[]{:S(2)}) collective-permute-start(s32[1536]{0:T(1024)S(1)} %convert_element_type.63), channel_id=1, source_target_pairs={{0,4},{4,0},{1,5},{5,1},{2,6},{6,2},{3,7},{7,3}} | collective-permute-start | bytes 18440 | tf_op jit(solution)/shard_map/while/body/ppermute | solution.py:36
  30.7 15.5 %copy-start.37 = (f32[1,7680]{1,0:T(1,128)S(1)}, f32[1,7680]{1,0:T(1,128)}, u32[]{:S(2)}) copy-start(f32[1,7680]{1,0:T(1,128)} %get-tuple-element.1198.bias_ref) | copy-start | bytes 92164 | tf_op jit(solution)/shard_map/while
  44.1 36.3 %collective-permute-start = (f32[384,768]{1,0:T(8,128)S(1)}, f32[384,768]{1,0:T(8,128)S(1)}, u32[]{:S(2)}, u32[]{:S(2)}) collective-permute-start(f32[384,768]{1,0:T(8,128)S(1)} %get-tuple-element.1052), channel_id=1, source_target_pairs={{0,4},{4,0},{1,5},{5,1},{2,6},{6,2},{3,7},{7,3}} | collective-permute-start | bytes 3538952 | tf_op jit(solution)/shard_map/while/body/ppermute | solution.py:36
  81.3 2.6 copy-start.14
  81.3 3.3 %copy-start.18 = (f32[1536]{0:T(1024)}, f32[1536]{0:T(1024)S(1)}, u32[]{:S(2)}) copy-start(f32[1536]{0:T(1024)S(1)} %get-tuple-element.1060) | copy-start | bytes 18436 | tf_op jit(solution)/shard_map/while
  82.0 2.6 copy-start.16
  82.0 1.9 collective-permute-start.4
  85.8 4.1 %collective-permute-start.5 = (f32[3,1536]{1,0:T(4,128)}, f32[3,1536]{1,0:T(4,128)}, u32[]{:S(2)}, u32[]{:S(2)}) collective-permute-start(f32[3,1536]{1,0:T(4,128)} %pad_maximum_fusion.16), channel_id=1, source_target_pairs={{0,2},{1,3},{2,0},{3,1},{4,6},{5,7},{6,4},{7,5}} | collective-permute-start | bytes 55304 | tf_op jit(solution)/shard_map/while/body/ppermute | solution.py:44
  88.0 43.8 %collective-permute-start.2 = (f32[384,768]{1,0:T(8,128)S(1)}, f32[384,768]{1,0:T(8,128)S(1)}, u32[]{:S(2)}, u32[]{:S(2)}) collective-permute-start(f32[384,768]{1,0:T(8,128)S(1)} %collective-permute-done.refs_0_), channel_id=1, source_target_pairs={{0,2},{1,3},{2,0},{3,1},{4,6},{5,7},{6,4},{7,5}} | collective-permute-start | bytes 3538952 | tf_op jit(solution)/shard_map/while/body/ppermute | solution.py:44
  88.5 43.3 %collective-permute-start.3 = (f32[384,768]{1,0:T(8,128)S(1)}, f32[384,768]{1,0:T(8,128)S(1)}, u32[]{:S(2)}, u32[]{:S(2)}) collective-permute-start(f32[384,768]{1,0:T(8,128)S(1)} %collective-permute-done.refs_0_), channel_id=1, source_target_pairs={{0,1},{1,0},{2,3},{3,2},{4,5},{5,4},{6,7},{7,6}} | collective-permute-start | bytes 3538952 | tf_op jit(solution)/shard_map/while/body/ppermute | solution.py:40
  93.9 40.8 %copy-start.51 = (s32[4]{0:T(128)S(1)}, s32[4]{0:T(128)}, u32[]{:S(2)}) copy-start(s32[4]{0:T(128)} %get-tuple-element.1206) | copy-start | bytes 52 | tf_op jit(solution)/shard_map/while
  93.9 40.8 %copy-start.33 = (s32[1536]{0:T(1024)S(1)}, s32[1536]{0:T(1024)}, u32[]{:S(2)}) copy-start(s32[1536]{0:T(1024)} %copy-done.32) | copy-start | bytes 18436 | tf_op jit(solution)/shard_map/while
  131.8 52.3 %copy-start.6 = (f32[1,7680]{1,0:T(1,128)}, f32[1,7680]{1,0:T(1,128)S(1)}, u32[]{:S(2)}) copy-start(f32[1,7680]{1,0:T(1,128)S(1)} %get-tuple-element.1104.db_own_ref) | copy-start | bytes 92164 | tf_op jit(solution)/shard_map/while
  131.8 2.9 collective-permute-start.6
  134.6 4.5 %collective-permute-start.7 = (f32[384,1536]{1,0:T(8,128)S(1)}, f32[384,1536]{1,0:T(8,128)S(1)}, u32[]{:S(2)}, u32[]{:S(2)}) collective-permute-start(f32[384,1536]{1,0:T(8,128)S(1)} %get-tuple-element.1071), channel_id=1, source_target_pairs={{0,1},{1,0},{2,3},{3,2},{4,5},{5,4},{6,7},{7,6}} | collective-permute-start | bytes 7077896 | tf_op jit(solution)/shard_map/while/body/ppermute | solution.py:40
  136.6 47.5 %copy-start = (bf16[1536,768]{1,0:T(8,128)(2,1)}, bf16[1536,768]{1,0:T(8,128)(2,1)S(1)}, u32[]{:S(2)}) copy-start(bf16[1536,768]{1,0:T(8,128)(2,1)S(1)} %get-tuple-element.1103.t_oth_ref) | copy-start | bytes 7077892 | tf_op jit(solution)/shard_map/while
  139.6 36.5 %collective-permute-start.8 = (f32[384,1024]{1,0:T(8,128)S(1)}, f32[384,1024]{1,0:T(8,128)S(1)}, u32[]{:S(2)}, u32[]{:S(2)}) collective-permute-start(f32[384,1024]{1,0:T(8,128)S(1)} %slice_add_fusion.9), channel_id=1, source_target_pairs={{0,2},{1,3},{2,0},{3,1},{4,6},{5,7},{6,4},{7,5}} | collective-permute-start | bytes 4718600 | tf_op jit(solution)/shard_map/while/body/ppermute | solution.py:44
  176.4 1.2 collective-permute-start.9
  177.7 6.3 %copy-start.25 = (f32[1536]{0:T(1024)S(1)}, f32[1536]{0:T(1024)}, u32[]{:S(2)}) copy-start(f32[1536]{0:T(1024)} %get-tuple-element.1098) | copy-start | bytes 18436 | tf_op jit(solution)/shard_map/while
  177.7 6.3 %copy-start.34 = (pred[120]{0:T(512)(128)(4,1)S(1)}, pred[120]{0:T(512)(128)(4,1)}, u32[]{:S(2)}) copy-start(pred[120]{0:T(512)(128)(4,1)} %broadcast_in_dim.326) | copy-start | bytes 364 | tf_op jit(solution)/shard_map/while
  177.7 3.8 %collective-permute-start.10 = (f32[3,1536]{1,0:T(4,128)S(1)}, f32[3,1536]{1,0:T(4,128)S(1)}, u32[]{:S(2)}, u32[]{:S(2)}) collective-permute-start(f32[3,1536]{1,0:T(4,128)S(1)} %pad_maximum_fusion.18), channel_id=1, source_target_pairs={{0,2},{1,3},{2,0},{3,1},{4,6},{5,7},{6,4},{7,5}} | collective-permute-start | bytes 55304 | tf_op jit(solution)/shard_map/while/body/ppermute | solution.py:44
  179.7 27.6 %copy-start.2 = (f32[384,1024]{1,0:T(8,128)}, f32[384,1024]{1,0:T(8,128)S(1)}, u32[]{:S(2)}) copy-start(f32[384,1024]{1,0:T(8,128)S(1)} %add.457.mine_a_ref) | copy-start | bytes 4718596 | tf_op jit(solution)/shard_map/while
  179.7 27.7 %collective-permute-start.12 = (f32[384,1024]{1,0:T(8,128)S(1)}, f32[384,1024]{1,0:T(8,128)S(1)}, u32[]{:S(2)}, u32[]{:S(2)}) collective-permute-start(f32[384,1024]{1,0:T(8,128)S(1)} %add.457.mine_a_ref), channel_id=1, source_target_pairs={{0,1},{1,0},{2,3},{3,2},{4,5},{5,4},{6,7},{7,6}} | collective-permute-start | bytes 4718600 | tf_op jit(solution)/shard_map/while/body/ppermute | solution.py:40
  182.3 25.1 %collective-permute-start.11 = (f32[384,512]{1,0:T(8,128)S(1)}, f32[384,512]{1,0:T(8,128)S(1)}, u32[]{:S(2)}, u32[]{:S(2)}) collective-permute-start(f32[384,512]{1,0:T(8,128)S(1)} %slice_add_fusion.10), channel_id=1, source_target_pairs={{0,2},{1,3},{2,0},{3,1},{4,6},{5,7},{6,4},{7,5}} | collective-permute-start | bytes 2359304 | tf_op jit(solution)/shard_map/while/body/ppermute | solution.py:44
  207.3 2.4 copy-start.15
  207.3 2.4 copy-start.17
  207.3 2.4 copy-start.19
  207.4 2.4 copy-start.26
  207.4 2.4 copy-start.27
  207.4 4.9 %copy-start.35 = (f32[1,768]{1,0:T(1,128)S(1)}, f32[1,768]{1,0:T(1,128)}, u32[]{:S(2)}) copy-start(f32[1,768]{1,0:T(1,128)} %get-tuple-element.1203.gamma_ref) | copy-start | bytes 9220 | tf_op jit(solution)/shard_map/while
  209.7 2.6 collective-permute-start.13
  215.1 13.5 %copy-start.1 = (bf16[1536,768]{1,0:T(8,128)(2,1)S(1)}, bf16[1536,768]{1,0:T(8,128)(2,1)}, u32[]{:S(2)}) copy-start(bf16[1536,768]{1,0:T(8,128)(2,1)} %copy-done) | copy-start | bytes 7077892 | tf_op jit(solution)/shard_map/while
  215.1 13.6 %copy-start.7 = (f32[1,7680]{1,0:T(1,128)S(1)}, f32[1,7680]{1,0:T(1,128)}, u32[]{:S(2)}) copy-start(f32[1,7680]{1,0:T(1,128)} %copy-done.6) | copy-start | bytes 92164 | tf_op jit(solution)/shard_map/while
  228.7 26.8 %copy-start.20 = (f32[1,7680]{1,0:T(1,128)S(1)}, f32[1,7680]{1,0:T(1,128)}, u32[]{:S(2)}) copy-start(f32[1,7680]{1,0:T(1,128)} %get-tuple-element.1157) | copy-start | bytes 92164 | tf_op jit(solution)/shard_map/while
  228.7 42.0 %copy-start.10 = (f32[200,768]{1,0:T(8,128)S(1)}, f32[200,768]{1,0:T(8,128)}, u32[]{:S(2)}) copy-start(f32[200,768]{1,0:T(8,128)} %get-tuple-element.1156) | copy-start | bytes 1843204 | tf_op jit(solution)/shard_map/while
  254.7 17.0 %copy-start.40 = (f32[8,768]{1,0:T(8,128)S(1)}, f32[8,768]{1,0:T(8,128)}, u32[]{:S(2)}) copy-start(f32[8,768]{1,0:T(8,128)} %copy-done.39) | copy-start | bytes 73732 | tf_op jit(solution)/shard_map/while
  254.7 17.0 %copy-start.42 = (s32[32]{0:T(128)S(1)}, s32[32]{0:T(128)}, u32[]{:S(2)}) copy-start(s32[32]{0:T(128)} %copy-done.41) | copy-start | bytes 388 | tf_op jit(solution)/shard_map/while
  254.8 17.0 %copy-start.44 = (s32[1,32]{1,0:T(1,128)S(1)}, s32[1,32]{1,0:T(1,128)}, u32[]{:S(2)}) copy-start(s32[1,32]{1,0:T(1,128)} %copy-done.43) | copy-start | bytes 388 | tf_op jit(solution)/shard_map/while
  254.8 17.0 %copy-start.48 = (f32[32,80]{1,0:T(8,128)S(1)}, f32[32,80]{1,0:T(8,128)}, u32[]{:S(2)}) copy-start(f32[32,80]{1,0:T(8,128)} %copy-done.47) | copy-start | bytes 30724 | tf_op jit(solution)/shard_map/while
  254.8 15.9 %collective-permute-start.14 = (f32[200,768]{1,0:T(8,128)S(1)}, f32[200,768]{1,0:T(8,128)S(1)}, u32[]{:S(2)}, u32[]{:S(2)}) collective-permute-start(f32[200,768]{1,0:T(8,128)S(1)} %constant_dynamic-slice_fusion.3), channel_id=1, source_target_pairs={{0,4},{4,0},{1,5},{5,1},{2,6},{6,2},{3,7},{7,3}} | collective-permute-start | bytes 1843208 | tf_op jit(solution)/shard_map/while/body/ppermute | solution.py:36
  255.5 15.4 %copy-start.21 = (f32[1,7680]{1,0:T(1,128)}, f32[1,7680]{1,0:T(1,128)S(1)}, u32[]{:S(2)}) copy-start(f32[1,7680]{1,0:T(1,128)S(1)} %maximum_add_fusion.3) | copy-start | bytes 92164 | tf_op jit(solution)/shard_map/while
  271.8 17.3 %collective-permute-start.16 = (f32[200,768]{1,0:T(8,128)}, f32[200,768]{1,0:T(8,128)S(1)}, u32[]{:S(2)}, u32[]{:S(2)}) collective-permute-start(f32[200,768]{1,0:T(8,128)} %get-tuple-element.397), channel_id=1, source_target_pairs={{0,2},{1,3},{2,0},{3,1},{4,6},{5,7},{6,4},{7,5}} | collective-permute-start | bytes 1843208 | tf_op jit(solution)/shard_map/ppermute | solution.py:44
  272.2 16.9 %collective-permute-start.17 = (f32[8,128]{1,0:T(8,128)S(1)}, f32[8,128]{1,0:T(8,128)S(1)}, u32[]{:S(2)}, u32[]{:S(2)}) collective-permute-start(f32[8,128]{1,0:T(8,128)S(1)} %broadcast_in_dim.226), channel_id=1, source_target_pairs={{0,4},{4,0},{1,5},{5,1},{2,6},{6,2},{3,7},{7,3}} | collective-permute-start | bytes 12296 | tf_op jit(solution)/shard_map/ppermute | solution.py:36
  273.4 15.7 %copy-start.12 = (f32[200,768]{1,0:T(8,128)S(1)}, f32[200,768]{1,0:T(8,128)}, u32[]{:S(2)}) copy-start(f32[200,768]{1,0:T(8,128)} %get-tuple-element.397) | copy-start | bytes 1843204
  290.2 3.1 %collective-permute-start.18 = (f32[2,200,768]{2,1,0:T(8,128)}, f32[2,200,768]{2,1,0:T(8,128)S(1)}, u32[]{:S(2)}, u32[]{:S(2)}) collective-permute-start(f32[2,200,768]{2,1,0:T(8,128)} %maximum_select_fusion.2), channel_id=1, source_target_pairs={{0,1},{1,0},{2,3},{3,2},{4,5},{5,4},{6,7},{7,6}} | collective-permute-start | bytes 3686408 | tf_op jit(solution)/shard_map/ppermute | solution.py:40
  (23 other events, 31.8 us)
